TPU v7x, 128 devices: a whole 4x4x4 slice. The times are simulated.
128 devices in a mesh: gx: 2 (over core), gy: 4 (over x), gz: 16 (over z, y).
Axes of the slice: x: 4, y: 4, z: 4, core: 2. Of those that a mesh axis runs over, the one named last changes fastest.
Arguments:
- right_side: float32 [64, 512, 1024], P('gx', 'gy', 'gz'), may hold values from -21 to 21, as said below
- conductivity: float32 [64, 512, 1024], P('gx', 'gy', 'gz'), may hold values from 0.25 to 1
- absorption: float32 [64, 512, 1024], P('gx', 'gy', 'gz'), may hold values from 0.5 to 2
Outputs:
- solution_field: float32 [64, 512, 1024], P('gx', 'gy', 'gz')
- residual: float32 [64, 512, 1024], P('gx', 'gy', 'gz')
Inputs may be any that keep to these rules, and one draw needn't show every extreme that they name: right_side lies within -21 and 21.
All inputs are finite; a program needn't handle non-finite values.
Results may differ from a plain program's by a relative error of at most 0.004.
Values sent between devices are 32-bit elements.
A program may use at most 128 MiB of HBM per device.

v0:
```python
import functools

import jax
import jax.numpy as jnp
from jax import lax
from jax.sharding import Mesh
from jax.sharding import PartitionSpec as P

ITERS = 10
GX_GY_GZ = ("gx", "gy", "gz_0", "gz_1")
GZ = ("gz_0", "gz_1")


def padded_2(shard, sides, width, wrap):
    edges = {}
    for axis, dim in sides:
        size, length = lax.axis_size(axis), shard.shape[dim]
        up = [(i, (i + 1) % size) for i in range(size if wrap else size - 1)]
        last = lax.slice_in_dim(shard, length - width, length, axis=dim)
        leading = lax.slice_in_dim(shard, 0, width, axis=dim)
        edges[dim] = lax.ppermute(last, axis, up), lax.ppermute(
            leading, axis, [(b, a) for a, b in up]
        )
    done = []
    for _, dim in sides:
        low, high = edges[dim]
        around = [(width, width) if d in done else (0, 0) for d in range(shard.ndim)]
        shard = jnp.concatenate([jnp.pad(low, around), shard, jnp.pad(high, around)], axis=dim)
        done.append(dim)
    return shard


def over_axes(shard, axes):
    return functools.reduce(lax.psum, axes, shard)


def coefficients(conductivity, absorption):
    padded = padded_2(conductivity, (("gx", 0), ("gy", 1), (GZ, 2)), 1, False)
    face_x = 0.5 * (padded[:-1, 1:-1, 1:-1] + padded[1:, 1:-1, 1:-1])
    face_y = 0.5 * (padded[1:-1, :-1, 1:-1] + padded[1:-1, 1:, 1:-1])
    face_z = 0.5 * (padded[1:-1, 1:-1, :-1] + padded[1:-1, 1:-1, 1:])
    total = (
        absorption
        + face_x[1:]
        + face_x[:-1]
        + face_y[:, 1:]
        + face_y[:, :-1]
        + face_z[:, :, 1:]
        + face_z[:, :, :-1]
    )
    return (face_x, face_y, face_z, total)


def operate(field, coeffs):
    face_x, face_y, face_z, total = coeffs
    padded = padded_2(field, (("gx", 0), ("gy", 1), (GZ, 2)), 1, False)
    beside = face_x[1:] * padded[2:, 1:-1, 1:-1] + face_x[:-1] * padded[:-2, 1:-1, 1:-1]
    beside = (
        beside + face_y[:, 1:] * padded[1:-1, 2:, 1:-1] + face_y[:, :-1] * padded[1:-1, :-2, 1:-1]
    )
    beside = (
        beside
        + face_z[:, :, 1:] * padded[1:-1, 1:-1, 2:]
        + face_z[:, :, :-1] * padded[1:-1, 1:-1, :-2]
    )
    return total * field - beside


def paired_dots(residual, precond, image):
    return (
        over_axes(jnp.sum(residual * precond), GX_GY_GZ),
        over_axes(jnp.sum(precond * image), GX_GY_GZ),
    )


def on_device(right_side, conductivity, absorption):
    coeffs = coefficients(conductivity, absorption)
    total = coeffs[3]
    solution_field = jnp.zeros_like(right_side)
    residual = right_side
    precond = residual / total
    image = operate(precond, coeffs)
    rho_now, product = paired_dots(residual, precond, image)
    step_size = rho_now / product
    direction = precond
    along = image
    for iteration in range(ITERS):
        solution_field = solution_field + step_size * direction
        residual = residual - step_size * along
        if iteration + 1 < ITERS:
            precond = residual / total
            image = operate(precond, coeffs)
            rho_next, product = paired_dots(residual, precond, image)
            mixing = rho_next / rho_now
            step_size = rho_next / (product - mixing * rho_next / step_size)
            direction = precond + mixing * direction
            along = image + mixing * along
            rho_now = rho_next
    return (solution_field, residual)


def solution(mesh):
    finer = Mesh(
        mesh.devices.reshape(mesh.shape["gx"], mesh.shape["gy"], 4, 4), ("gx", "gy", "gz_0", "gz_1")
    )
    in_specs = (P("gx", "gy", GZ), P("gx", "gy", GZ), P("gx", "gy", GZ))
    out_specs = (P("gx", "gy", GZ), P("gx", "gy", GZ))
    return jax.shard_map(
        on_device, mesh=finer, in_specs=in_specs, out_specs=out_specs, check_vma=False
    )
```

profile of v0, /device:TPU:8, one launch (start us, length us, event | category | flops | bytes accessed | tf_op | source)
XLA Modules:
  0.0 790.9 jit_solution(5665525134292880309)
XLA Ops:
  66.6 10.5 %all-reduce.73 = (f32[]{:T(128)}, f32[]{:T(128)}) all-reduce(f32[]{:T(128)} %get-tuple-element.106, f32[]{:T(128)} %get-tuple-element.107), channel_id=1, replica_groups=mesh['gx'=2,'gy'=4,'gz_0'=4,'gz_1'=4] {'gy'}, use_global_device_ids=true, to_apply=%region_2.3 | all-reduce | flops 2 | bytes 16 | tf_op jit(solution)/shard_map/psum | solution.py:34
  77.1 12.5 %all-reduce.63 = (f32[]{:T(128)}, f32[]{:T(128)}) all-reduce(f32[]{:T(128)} %get-tuple-element.86, f32[]{:T(128)} %get-tuple-element.87), channel_id=1, replica_groups=mesh['gx'=2,'gy'=4,'gz_0'=4,'gz_1'=4] {'gz_0'}, use_global_device_ids=true, to_apply=%region_3.4 | all-reduce | flops 2 | bytes 16 | tf_op jit(solution)/shard_map/psum | solution.py:34
  89.6 12.0 %all-reduce.53 = (f32[]{:T(128)}, f32[]{:T(128)}) all-reduce(f32[]{:T(128)} %get-tuple-element.66, f32[]{:T(128)} %get-tuple-element.67), channel_id=1, replica_groups=mesh['gx'=2,'gy'=4,'gz_0'=4,'gz_1'=4] {'gz_1'}, use_global_device_ids=true, to_apply=%region_4.5 | all-reduce | flops 2 | bytes 16 | tf_op jit(solution)/shard_map/psum | solution.py:34
  143.4 10.5 %all-reduce.72 = (f32[]{:T(128)}, f32[]{:T(128)}) all-reduce(f32[]{:T(128)} %get-tuple-element.104, f32[]{:T(128)} %get-tuple-element.105), channel_id=1, replica_groups=mesh['gx'=2,'gy'=4,'gz_0'=4,'gz_1'=4] {'gy'}, use_global_device_ids=true, to_apply=%region_12.13 | all-reduce | flops 2 | bytes 16 | tf_op jit(solution)/shard_map/psum | solution.py:34
  162.3 12.4 %all-reduce.52 = (f32[]{:T(128)}, f32[]{:T(128)}) all-reduce(f32[]{:T(128)} %get-tuple-element.64, f32[]{:T(128)} %get-tuple-element.65), channel_id=1, replica_groups=mesh['gx'=2,'gy'=4,'gz_0'=4,'gz_1'=4] {'gz_1'}, use_global_device_ids=true, to_apply=%region_14.15 | all-reduce | flops 2 | bytes 16 | tf_op jit(solution)/shard_map/psum | solution.py:34
  219.4 10.6 %all-reduce.71 = (f32[]{:T(128)}, f32[]{:T(128)}) all-reduce(f32[]{:T(128)} %get-tuple-element.102, f32[]{:T(128)} %get-tuple-element.103), channel_id=1, replica_groups=mesh['gx'=2,'gy'=4,'gz_0'=4,'gz_1'=4] {'gy'}, use_global_device_ids=true, to_apply=%region_22.23 | all-reduce | flops 2 | bytes 16 | tf_op jit(solution)/shard_map/psum | solution.py:34
  238.4 11.0 %all-reduce.51 = (f32[]{:T(128)}, f32[]{:T(128)}) all-reduce(f32[]{:T(128)} %get-tuple-element.62, f32[]{:T(128)} %get-tuple-element.63), channel_id=1, replica_groups=mesh['gx'=2,'gy'=4,'gz_0'=4,'gz_1'=4] {'gz_1'}, use_global_device_ids=true, to_apply=%region_24.25 | all-reduce | flops 2 | bytes 16 | tf_op jit(solution)/shard_map/psum | solution.py:34
  295.0 10.6 %all-reduce.70 = (f32[]{:T(128)}, f32[]{:T(128)}) all-reduce(f32[]{:T(128)} %get-tuple-element.100, f32[]{:T(128)} %get-tuple-element.101), channel_id=1, replica_groups=mesh['gx'=2,'gy'=4,'gz_0'=4,'gz_1'=4] {'gy'}, use_global_device_ids=true, to_apply=%region_32.33 | all-reduce | flops 2 | bytes 16 | tf_op jit(solution)/shard_map/psum | solution.py:34
  314.0 11.9 %all-reduce.50 = (f32[]{:T(128)}, f32[]{:T(128)}) all-reduce(f32[]{:T(128)} %get-tuple-element.60, f32[]{:T(128)} %get-tuple-element.61), channel_id=1, replica_groups=mesh['gx'=2,'gy'=4,'gz_0'=4,'gz_1'=4] {'gz_1'}, use_global_device_ids=true, to_apply=%region_34.35 | all-reduce | flops 2 | bytes 16 | tf_op jit(solution)/shard_map/psum | solution.py:34
  357.5 10.0 %multiply_reduce_fusion.10 = (f32[]{:T(128)}, f32[]{:T(128)}, f32[32,128,64]{1,2,0:T(8,128)}) fusion(f32[32,128,64]{1,2,0:T(8,128)} %copy-done.17, f32[32,128,64]{1,2,0:T(8,128)} %get-tuple-element.127, f32[34,1,64]{1,2,0:T(8,128)S(1)} %pad.154, f32[1,128,64]{1,2,0:T(8,128)S(1)} %collective-permute-done.30, f32[1,128,64]{1,2,0:T(8,128)S(1)} %collective-permute-done.31, ...), kind=kLoop, calls=%fused_computation.362 | loop fusion | flops 10747902 | bytes 10601480 | tf_op jit(solution)/shard_map/reduce_sum | solution.py:72
  370.6 10.7 %all-reduce.69 = (f32[]{:T(128)}, f32[]{:T(128)}) all-reduce(f32[]{:T(128)} %get-tuple-element.98, f32[]{:T(128)} %get-tuple-element.99), channel_id=1, replica_groups=mesh['gx'=2,'gy'=4,'gz_0'=4,'gz_1'=4] {'gy'}, use_global_device_ids=true, to_apply=%region_42.43 | all-reduce | flops 2 | bytes 16 | tf_op jit(solution)/shard_map/psum | solution.py:34
  389.7 11.1 %all-reduce.49 = (f32[]{:T(128)}, f32[]{:T(128)}) all-reduce(f32[]{:T(128)} %get-tuple-element.58, f32[]{:T(128)} %get-tuple-element.59), channel_id=1, replica_groups=mesh['gx'=2,'gy'=4,'gz_0'=4,'gz_1'=4] {'gz_1'}, use_global_device_ids=true, to_apply=%region_44.45 | all-reduce | flops 2 | bytes 16 | tf_op jit(solution)/shard_map/psum | solution.py:34
  433.8 10.0 %multiply_reduce_fusion.8 = (f32[]{:T(128)}, f32[]{:T(128)}, f32[32,128,64]{1,2,0:T(8,128)}) fusion(f32[32,128,64]{1,2,0:T(8,128)} %copy-done.13, f32[32,128,64]{1,2,0:T(8,128)} %get-tuple-element.123, f32[34,1,64]{1,2,0:T(8,128)S(1)} %pad.158, f32[1,128,64]{1,2,0:T(8,128)S(1)} %collective-permute-done.36, f32[1,128,64]{1,2,0:T(8,128)S(1)} %collective-permute-done.37, ...), kind=kLoop, calls=%fused_computation.358 | loop fusion | flops 10747902 | bytes 10601480 | tf_op jit(solution)/shard_map/reduce_sum | solution.py:72
  447.0 10.5 %all-reduce.68 = (f32[]{:T(128)}, f32[]{:T(128)}) all-reduce(f32[]{:T(128)} %get-tuple-element.96, f32[]{:T(128)} %get-tuple-element.97), channel_id=1, replica_groups=mesh['gx'=2,'gy'=4,'gz_0'=4,'gz_1'=4] {'gy'}, use_global_device_ids=true, to_apply=%region_52.53 | all-reduce | flops 2 | bytes 16 | tf_op jit(solution)/shard_map/psum | solution.py:34
  465.9 11.9 %all-reduce.48 = (f32[]{:T(128)}, f32[]{:T(128)}) all-reduce(f32[]{:T(128)} %get-tuple-element.56, f32[]{:T(128)} %get-tuple-element.57), channel_id=1, replica_groups=mesh['gx'=2,'gy'=4,'gz_0'=4,'gz_1'=4] {'gz_1'}, use_global_device_ids=true, to_apply=%region_54.55 | all-reduce | flops 2 | bytes 16 | tf_op jit(solution)/shard_map/psum | solution.py:34
  522.0 10.6 %all-reduce.67 = (f32[]{:T(128)}, f32[]{:T(128)}) all-reduce(f32[]{:T(128)} %get-tuple-element.94, f32[]{:T(128)} %get-tuple-element.95), channel_id=1, replica_groups=mesh['gx'=2,'gy'=4,'gz_0'=4,'gz_1'=4] {'gy'}, use_global_device_ids=true, to_apply=%region_62.63 | all-reduce | flops 2 | bytes 16 | tf_op jit(solution)/shard_map/psum | solution.py:34
  540.9 11.3 %all-reduce.47 = (f32[]{:T(128)}, f32[]{:T(128)}) all-reduce(f32[]{:T(128)} %get-tuple-element.54, f32[]{:T(128)} %get-tuple-element.55), channel_id=1, replica_groups=mesh['gx'=2,'gy'=4,'gz_0'=4,'gz_1'=4] {'gz_1'}, use_global_device_ids=true, to_apply=%region_64.65 | all-reduce | flops 2 | bytes 16 | tf_op jit(solution)/shard_map/psum | solution.py:34
  597.3 10.6 %all-reduce.66 = (f32[]{:T(128)}, f32[]{:T(128)}) all-reduce(f32[]{:T(128)} %get-tuple-element.92, f32[]{:T(128)} %get-tuple-element.93), channel_id=1, replica_groups=mesh['gx'=2,'gy'=4,'gz_0'=4,'gz_1'=4] {'gy'}, use_global_device_ids=true, to_apply=%region_72.73 | all-reduce | flops 2 | bytes 16 | tf_op jit(solution)/shard_map/psum | solution.py:34
  616.2 11.9 %all-reduce.46 = (f32[]{:T(128)}, f32[]{:T(128)}) all-reduce(f32[]{:T(128)} %get-tuple-element.52, f32[]{:T(128)} %get-tuple-element.53), channel_id=1, replica_groups=mesh['gx'=2,'gy'=4,'gz_0'=4,'gz_1'=4] {'gz_1'}, use_global_device_ids=true, to_apply=%region_74.75 | all-reduce | flops 2 | bytes 16 | tf_op jit(solution)/shard_map/psum | solution.py:34
  672.1 10.5 %all-reduce.65 = (f32[]{:T(128)}, f32[]{:T(128)}) all-reduce(f32[]{:T(128)} %get-tuple-element.90, f32[]{:T(128)} %get-tuple-element.91), channel_id=1, replica_groups=mesh['gx'=2,'gy'=4,'gz_0'=4,'gz_1'=4] {'gy'}, use_global_device_ids=true, to_apply=%region_82.83 | all-reduce | flops 2 | bytes 16 | tf_op jit(solution)/shard_map/psum | solution.py:34
  691.0 11.0 %all-reduce.45 = (f32[]{:T(128)}, f32[]{:T(128)}) all-reduce(f32[]{:T(128)} %get-tuple-element.50, f32[]{:T(128)} %get-tuple-element.51), channel_id=1, replica_groups=mesh['gx'=2,'gy'=4,'gz_0'=4,'gz_1'=4] {'gz_1'}, use_global_device_ids=true, to_apply=%region_84.85 | all-reduce | flops 2 | bytes 16 | tf_op jit(solution)/shard_map/psum | solution.py:34
  734.2 10.3 %multiply_reduce_fusion = (f32[]{:T(128)}, f32[]{:T(128)}, f32[32,128,64]{1,2,0:T(8,128)}) fusion(f32[32,128,64]{1,2,0:T(8,128)} %copy-done.20, f32[32,128,64]{1,2,0:T(8,128)} %get-tuple-element.113, f32[32,128,64]{1,2,0:T(8,128)} %get-tuple-element.110, f32[]{:T(128)S(6)} %div.147, f32[34,1,64]{1,2,0:T(8,128)S(1)} %pad.174, ...), kind=kLoop, calls=%fused_computation.342 | loop fusion | flops 11272190 | bytes 11650060 | tf_op jit(solution)/shard_map/reduce_sum | solution.py:72
  747.7 10.7 %all-reduce.64 = (f32[]{:T(128)}, f32[]{:T(128)}) all-reduce(f32[]{:T(128)} %get-tuple-element.88, f32[]{:T(128)} %get-tuple-element.89), channel_id=1, replica_groups=mesh['gx'=2,'gy'=4,'gz_0'=4,'gz_1'=4] {'gy'}, use_global_device_ids=true, to_apply=%region_92.93 | all-reduce | flops 2 | bytes 16 | tf_op jit(solution)/shard_map/psum | solution.py:34
  766.8 11.9 %all-reduce.44 = (f32[]{:T(128)}, f32[]{:T(128)}) all-reduce(f32[]{:T(128)} %get-tuple-element.48, f32[]{:T(128)} %get-tuple-element.49), channel_id=1, replica_groups=mesh['gx'=2,'gy'=4,'gz_0'=4,'gz_1'=4] {'gz_1'}, use_global_device_ids=true, to_apply=%region_94.95 | all-reduce | flops 2 | bytes 16 | tf_op jit(solution)/shard_map/psum | solution.py:34
  (331 shorter events, 486.8 us)
Async XLA Ops:
  1.4 18.6 %collective-permute-start = (f32[1,128,64]{1,2,0:T(8,128)S(1)}, f32[1,128,64]{1,2,0:T(8,128)S(1)}, u32[]{:S(2)}, u32[]{:S(2)}) collective-permute-start(f32[1,128,64]{1,2,0:T(8,128)S(1)} %get-tuple-element.206), channel_id=1, source_target_pairs={{0,64},{1,65},{2,66},{3,67},{4,68},{5,69},{6,70},{7,71},{8,72},{9,... | collective-permute-start | bytes 98312 | tf_op jit(solution)/shard_map/ppermute | solution.py:21
  28.3 25.1 %collective-permute-start.7 = (f32[1,128,64]{1,2,0:T(8,128)S(1)}, f32[1,128,64]{1,2,0:T(8,128)S(1)}, u32[]{:S(2)}, u32[]{:S(2)}) collective-permute-start(f32[1,128,64]{1,2,0:T(8,128)S(1)} %get-tuple-element.199), channel_id=1, source_target_pairs={{0,64},{1,65},{2,66},{3,67},{4,68},{5,69},{6,70},{7,71},{8,72},{9,... | collective-permute-start | bytes 98312 | tf_op jit(solution)/shard_map/ppermute | solution.py:21
  31.1 22.3 %collective-permute-start.6 = (f32[1,128,64]{1,2,0:T(8,128)S(1)}, f32[1,128,64]{1,2,0:T(8,128)S(1)}, u32[]{:S(2)}, u32[]{:S(2)}) collective-permute-start(f32[1,128,64]{1,2,0:T(8,128)S(1)} %get-tuple-element.200), channel_id=1, source_target_pairs={{64,0},{65,1},{66,2},{67,3},{68,4},{69,5},{70,6},{71,7},{72,8},{73... | collective-permute-start | bytes 98312 | tf_op jit(solution)/shard_map/ppermute | solution.py:21
  107.3 22.7 %collective-permute-start.13 = (f32[1,128,64]{1,2,0:T(8,128)S(1)}, f32[1,128,64]{1,2,0:T(8,128)S(1)}, u32[]{:S(2)}, u32[]{:S(2)}) collective-permute-start(f32[1,128,64]{1,2,0:T(8,128)S(1)} %get-tuple-element.193), channel_id=1, source_target_pairs={{0,64},{1,65},{2,66},{3,67},{4,68},{5,69},{6,70},{7,71},{8,72},{9,... | collective-permute-start | bytes 98312 | tf_op jit(solution)/shard_map/ppermute | solution.py:21
  108.6 21.4 %collective-permute-start.12 = (f32[1,128,64]{1,2,0:T(8,128)S(1)}, f32[1,128,64]{1,2,0:T(8,128)S(1)}, u32[]{:S(2)}, u32[]{:S(2)}) collective-permute-start(f32[1,128,64]{1,2,0:T(8,128)S(1)} %get-tuple-element.194), channel_id=1, source_target_pairs={{64,0},{65,1},{66,2},{67,3},{68,4},{69,5},{70,6},{71,7},{72,8},{73... | collective-permute-start | bytes 98312 | tf_op jit(solution)/shard_map/ppermute | solution.py:21
  184.3 22.1 %collective-permute-start.19 = (f32[1,128,64]{1,2,0:T(8,128)S(1)}, f32[1,128,64]{1,2,0:T(8,128)S(1)}, u32[]{:S(2)}, u32[]{:S(2)}) collective-permute-start(f32[1,128,64]{1,2,0:T(8,128)S(1)} %get-tuple-element.187), channel_id=1, source_target_pairs={{0,64},{1,65},{2,66},{3,67},{4,68},{5,69},{6,70},{7,71},{8,72},{9,... | collective-permute-start | bytes 98312 | tf_op jit(solution)/shard_map/ppermute | solution.py:21
  185.6 20.8 %collective-permute-start.18 = (f32[1,128,64]{1,2,0:T(8,128)S(1)}, f32[1,128,64]{1,2,0:T(8,128)S(1)}, u32[]{:S(2)}, u32[]{:S(2)}) collective-permute-start(f32[1,128,64]{1,2,0:T(8,128)S(1)} %get-tuple-element.188), channel_id=1, source_target_pairs={{64,0},{65,1},{66,2},{67,3},{68,4},{69,5},{70,6},{71,7},{72,8},{73... | collective-permute-start | bytes 98312 | tf_op jit(solution)/shard_map/ppermute | solution.py:21
  190.4 16.0 %collective-permute-start.23 = (f32[32,128,1]{1,0,2:T(8,128)S(1)}, f32[32,128,1]{1,0,2:T(8,128)S(1)}, u32[]{:S(2)}, u32[]{:S(2)}) collective-permute-start(f32[32,128,1]{1,0,2:T(8,128)S(1)} %bitcast.81), channel_id=1, source_target_pairs={{0,1},{1,2},{2,3},{3,4},{4,5},{5,6},{6,7},{7,8},{8,9},{9,10},{10,1... | collective-permute-start | bytes 49160 | tf_op jit(solution)/shard_map/ppermute | solution.py:21
  259.2 22.4 %collective-permute-start.25 = (f32[1,128,64]{1,2,0:T(8,128)S(1)}, f32[1,128,64]{1,2,0:T(8,128)S(1)}, u32[]{:S(2)}, u32[]{:S(2)}) collective-permute-start(f32[1,128,64]{1,2,0:T(8,128)S(1)} %get-tuple-element.181), channel_id=1, source_target_pairs={{0,64},{1,65},{2,66},{3,67},{4,68},{5,69},{6,70},{7,71},{8,72},{9,... | collective-permute-start | bytes 98312 | tf_op jit(solution)/shard_map/ppermute | solution.py:21
  260.5 21.2 %collective-permute-start.24 = (f32[1,128,64]{1,2,0:T(8,128)S(1)}, f32[1,128,64]{1,2,0:T(8,128)S(1)}, u32[]{:S(2)}, u32[]{:S(2)}) collective-permute-start(f32[1,128,64]{1,2,0:T(8,128)S(1)} %get-tuple-element.182), channel_id=1, source_target_pairs={{64,0},{65,1},{66,2},{67,3},{68,4},{69,5},{70,6},{71,7},{72,8},{73... | collective-permute-start | bytes 98312 | tf_op jit(solution)/shard_map/ppermute | solution.py:21
  335.0 22.1 %collective-permute-start.31 = (f32[1,128,64]{1,2,0:T(8,128)S(1)}, f32[1,128,64]{1,2,0:T(8,128)S(1)}, u32[]{:S(2)}, u32[]{:S(2)}) collective-permute-start(f32[1,128,64]{1,2,0:T(8,128)S(1)} %get-tuple-element.175), channel_id=1, source_target_pairs={{0,64},{1,65},{2,66},{3,67},{4,68},{5,69},{6,70},{7,71},{8,72},{9,... | collective-permute-start | bytes 98312 | tf_op jit(solution)/shard_map/ppermute | solution.py:21
  336.3 20.8 %collective-permute-start.30 = (f32[1,128,64]{1,2,0:T(8,128)S(1)}, f32[1,128,64]{1,2,0:T(8,128)S(1)}, u32[]{:S(2)}, u32[]{:S(2)}) collective-permute-start(f32[1,128,64]{1,2,0:T(8,128)S(1)} %get-tuple-element.176), channel_id=1, source_target_pairs={{64,0},{65,1},{66,2},{67,3},{68,4},{69,5},{70,6},{71,7},{72,8},{73... | collective-permute-start | bytes 98312 | tf_op jit(solution)/shard_map/ppermute | solution.py:21
  341.0 16.0 %collective-permute-start.35 = (f32[32,128,1]{1,0,2:T(8,128)S(1)}, f32[32,128,1]{1,0,2:T(8,128)S(1)}, u32[]{:S(2)}, u32[]{:S(2)}) collective-permute-start(f32[32,128,1]{1,0,2:T(8,128)S(1)} %bitcast.83), channel_id=1, source_target_pairs={{0,1},{1,2},{2,3},{3,4},{4,5},{5,6},{6,7},{7,8},{8,9},{9,10},{10,1... | collective-permute-start | bytes 49160 | tf_op jit(solution)/shard_map/ppermute | solution.py:21
  410.9 22.4 %collective-permute-start.37 = (f32[1,128,64]{1,2,0:T(8,128)S(1)}, f32[1,128,64]{1,2,0:T(8,128)S(1)}, u32[]{:S(2)}, u32[]{:S(2)}) collective-permute-start(f32[1,128,64]{1,2,0:T(8,128)S(1)} %get-tuple-element.169), channel_id=1, source_target_pairs={{0,64},{1,65},{2,66},{3,67},{4,68},{5,69},{6,70},{7,71},{8,72},{9,... | collective-permute-start | bytes 98312 | tf_op jit(solution)/shard_map/ppermute | solution.py:21
  412.2 21.2 %collective-permute-start.36 = (f32[1,128,64]{1,2,0:T(8,128)S(1)}, f32[1,128,64]{1,2,0:T(8,128)S(1)}, u32[]{:S(2)}, u32[]{:S(2)}) collective-permute-start(f32[1,128,64]{1,2,0:T(8,128)S(1)} %get-tuple-element.170), channel_id=1, source_target_pairs={{64,0},{65,1},{66,2},{67,3},{68,4},{69,5},{70,6},{71,7},{72,8},{73... | collective-permute-start | bytes 98312 | tf_op jit(solution)/shard_map/ppermute | solution.py:21
  486.8 22.0 %collective-permute-start.43 = (f32[1,128,64]{1,2,0:T(8,128)S(1)}, f32[1,128,64]{1,2,0:T(8,128)S(1)}, u32[]{:S(2)}, u32[]{:S(2)}) collective-permute-start(f32[1,128,64]{1,2,0:T(8,128)S(1)} %get-tuple-element.163), channel_id=1, source_target_pairs={{0,64},{1,65},{2,66},{3,67},{4,68},{5,69},{6,70},{7,71},{8,72},{9,... | collective-permute-start | bytes 98312 | tf_op jit(solution)/shard_map/ppermute | solution.py:21
  488.1 20.8 %collective-permute-start.42 = (f32[1,128,64]{1,2,0:T(8,128)S(1)}, f32[1,128,64]{1,2,0:T(8,128)S(1)}, u32[]{:S(2)}, u32[]{:S(2)}) collective-permute-start(f32[1,128,64]{1,2,0:T(8,128)S(1)} %get-tuple-element.164), channel_id=1, source_target_pairs={{64,0},{65,1},{66,2},{67,3},{68,4},{69,5},{70,6},{71,7},{72,8},{73... | collective-permute-start | bytes 98312 | tf_op jit(solution)/shard_map/ppermute | solution.py:21
  562.1 22.4 %collective-permute-start.49 = (f32[1,128,64]{1,2,0:T(8,128)S(1)}, f32[1,128,64]{1,2,0:T(8,128)S(1)}, u32[]{:S(2)}, u32[]{:S(2)}) collective-permute-start(f32[1,128,64]{1,2,0:T(8,128)S(1)} %get-tuple-element.157), channel_id=1, source_target_pairs={{0,64},{1,65},{2,66},{3,67},{4,68},{5,69},{6,70},{7,71},{8,72},{9,... | collective-permute-start | bytes 98312 | tf_op jit(solution)/shard_map/ppermute | solution.py:21
  563.3 21.1 %collective-permute-start.48 = (f32[1,128,64]{1,2,0:T(8,128)S(1)}, f32[1,128,64]{1,2,0:T(8,128)S(1)}, u32[]{:S(2)}, u32[]{:S(2)}) collective-permute-start(f32[1,128,64]{1,2,0:T(8,128)S(1)} %get-tuple-element.158), channel_id=1, source_target_pairs={{64,0},{65,1},{66,2},{67,3},{68,4},{69,5},{70,6},{71,7},{72,8},{73... | collective-permute-start | bytes 98312 | tf_op jit(solution)/shard_map/ppermute | solution.py:21
  636.9 22.1 %collective-permute-start.55 = (f32[1,128,64]{1,2,0:T(8,128)S(1)}, f32[1,128,64]{1,2,0:T(8,128)S(1)}, u32[]{:S(2)}, u32[]{:S(2)}) collective-permute-start(f32[1,128,64]{1,2,0:T(8,128)S(1)} %get-tuple-element.151), channel_id=1, source_target_pairs={{0,64},{1,65},{2,66},{3,67},{4,68},{5,69},{6,70},{7,71},{8,72},{9,... | collective-permute-start | bytes 98312 | tf_op jit(solution)/shard_map/ppermute | solution.py:21
  638.2 20.8 %collective-permute-start.54 = (f32[1,128,64]{1,2,0:T(8,128)S(1)}, f32[1,128,64]{1,2,0:T(8,128)S(1)}, u32[]{:S(2)}, u32[]{:S(2)}) collective-permute-start(f32[1,128,64]{1,2,0:T(8,128)S(1)} %get-tuple-element.152), channel_id=1, source_target_pairs={{64,0},{65,1},{66,2},{67,3},{68,4},{69,5},{70,6},{71,7},{72,8},{73... | collective-permute-start | bytes 98312 | tf_op jit(solution)/shard_map/ppermute | solution.py:21
  711.4 22.5 %collective-permute-start.61 = (f32[1,128,64]{1,2,0:T(8,128)S(1)}, f32[1,128,64]{1,2,0:T(8,128)S(1)}, u32[]{:S(2)}, u32[]{:S(2)}) collective-permute-start(f32[1,128,64]{1,2,0:T(8,128)S(1)} %get-tuple-element.145), channel_id=1, source_target_pairs={{0,64},{1,65},{2,66},{3,67},{4,68},{5,69},{6,70},{7,71},{8,72},{9,... | collective-permute-start | bytes 98312 | tf_op jit(solution)/shard_map/ppermute | solution.py:21
  712.6 21.2 %collective-permute-start.60 = (f32[1,128,64]{1,2,0:T(8,128)S(1)}, f32[1,128,64]{1,2,0:T(8,128)S(1)}, u32[]{:S(2)}, u32[]{:S(2)}) collective-permute-start(f32[1,128,64]{1,2,0:T(8,128)S(1)} %get-tuple-element.146), channel_id=1, source_target_pairs={{64,0},{65,1},{66,2},{67,3},{68,4},{69,5},{70,6},{71,7},{72,8},{73... | collective-permute-start | bytes 98312 | tf_op jit(solution)/shard_map/ppermute | solution.py:21
  717.8 16.0 %collective-permute-start.65 = (f32[32,128,1]{1,0,2:T(8,128)S(1)}, f32[32,128,1]{1,0,2:T(8,128)S(1)}, u32[]{:S(2)}, u32[]{:S(2)}) collective-permute-start(f32[32,128,1]{1,0,2:T(8,128)S(1)} %bitcast.78), channel_id=1, source_target_pairs={{0,1},{1,2},{2,3},{3,4},{4,5},{5,6},{6,7},{7,8},{8,9},{9,10},{10,1... | collective-permute-start | bytes 49160 | tf_op jit(solution)/shard_map/ppermute | solution.py:21
  (70 other events, 546.0 us)
where the time goes:
time: 803 us; the launch traced here: 791 us
  blocking collectives  341 us (42%)
  other arithmetic  143 us (18%)
  starting transfers between devices  136 us (17%)
  local copies, waits for them, and re-layouts  126 us (16%)
  between operations  39.1 us (5%)
    psum x40, blocking collectives, over_axes(): return functools.reduce(lax.psum, axes, shard)  341 us
    reduce_sum x10, other arithmetic, paired_dots(): jnp.sum(precond * image)  97.7 us
    ppermute x33, starting transfers between devices, padded_2(): lax.ppermute(leading, axis, [(b, a) for a, b in up])  68.5 us
    ppermute x33, starting transfers between devices, padded_2(): lax.ppermute(last, axis, up)  67.3 us
    slice x32, local copies, waits for them, and re-layouts, padded_2(): last = lax.slice_in_dim(shard, length - width, length, axis=dim)  34.8 us
    div x10, other arithmetic, on_device(): precond = residual / total  33.9 us
    pad x11, local copies, waits for them, and re-layouts, padded_2(): jnp.pad(low, around)  24.1 us
    slice x21, local copies, waits for them, and re-layouts, padded_2(): leading = lax.slice_in_dim(shard, 0, width, axis=dim)  16.9 us
  transfers between devices with their start and end apart: 66, of which 11 were waited for; matrix products, arithmetic and copies ran while one was open for 13% of the time, Pallas kernels for 0%

commit v1 on v0

v1 whole, which is shorter than its diff:
```python
import functools

import jax
import jax.numpy as jnp
from jax import lax
from jax.experimental import pallas as pl
from jax.experimental.pallas import tpu as pltpu
from jax.sharding import PartitionSpec as P

F32 = jnp.float32
MESH = pl.DeviceIdType.MESH
STEPS = 5
RHO = 0.65
LANES = 128


def added(p, q, scale=None):
    out = dict(p)
    for k, v in q.items():
        w = v if scale is None else scale * v
        out[k] = out[k] + w if k in out else w
    return out


def form(p, q, gram):
    total = None
    for i, a in p.items():
        row = None
        for j, b in q.items():
            g = gram(i, j)
            if g is not None:
                row = g * b if row is None else row + g * b
        if row is not None:
            total = a * row if total is None else total + a * row
    return total


def first_block(mu, one):
    def gram(i, j):
        return 0.5 * (mu[i + j] + mu[abs(i - j)])

    def times(q):
        out = {}
        for k, v in q.items():
            for kk in (k + 1, abs(k - 1)):
                h = 0.5 * v
                out[kk] = out[kk] + h if kk in out else h
        return out

    p, q, x, rho = {0: one}, {0: one}, {}, mu[0]
    for it in range(STEPS):
        image = added(q, times(q), -RHO)
        step = rho / form(q, image, gram)
        x = added(x, q, step)
        p = added(p, image, -step)
        if it + 1 < STEPS:
            new = form(p, p, gram)
            q = added(p, q, new / rho)
            rho = new
    return x, p, q, rho


def second_block(nu, c, x5, q4, rho4, mu, one):
    n = STEPS
    inverse = one / c[n]
    cross = {}

    def own(i, j):
        return 0.5 * (nu[i + j] + nu[abs(i - j)])

    def last(j):
        acc = own(j, 0)
        for k in range(n):
            if cross[(j, k)] is not None:
                acc = acc - c[k] * cross[(j, k)]
        return inverse * acc

    def plus(a, b, sign=1.0):
        if b is None:
            return a
        if a is None:
            return sign * b
        return a + sign * b

    for k in range(n):
        cross[(0, k)] = None
    cross[(0, n)] = last(0)
    for j in range(1, n + 1):
        for k in range(n):
            both = plus(cross[(j - 1, k + 1)], cross[(j - 1, abs(k - 1))])
            if j == 1:
                cross[(j, k)] = None if both is None else 0.5 * both
            else:
                cross[(j, k)] = plus(both, cross[(j - 2, k)], -1.0)
        if j < n:
            cross[(j, n)] = last(j)

    def gram(a, b):
        if a[0] == b[0]:
            m = nu if a[0] == "y" else mu
            return 0.5 * (m[a[1] + b[1]] + m[abs(a[1] - b[1])])
        if a[0] == "t":
            a, b = b, a
        return cross[(a[1], b[1])]

    def times(q):
        out = {}

        def put(k, v):
            out[k] = out[k] + v if k in out else v

        for (s, k), v in q.items():
            h = 0.5 * v
            put((s, abs(k - 1)), h)
            if s == "t" and k == n - 1:
                w = h * inverse
                put(("y", 0), w)
                for kk in range(n):
                    put(("t", kk), -(w * c[kk]))
            else:
                put((s, k + 1), h)
        return out

    rho = nu[0]
    p = {("y", 0): one}
    x = {("t", k): v for k, v in x5.items()}
    q = added(p, {("t", k): v for k, v in q4.items()}, rho / rho4)
    for it in range(n):
        image = added(q, times(q), -RHO)
        step = rho / form(q, image, gram)
        x = added(x, q, step)
        p = added(p, image, -step)
        if it + 1 < n:
            new = form(p, p, gram)
            q = added(p, q, new / rho)
            rho = new
    return x, p


def kernel(nx, nz, sizes, r_hbm, c_hbm, a_hbm, x_hbm, o_hbm,
           cond, absorb, diag, weight, fx, fy, fz, ey, halo, field, zsend, zrecv, ysend, yrecv,
           part1, part2, coef, xout, rout,
           load_sem, store_sem, face_send, face_recv, sum1_send, sum1_recv, sum2_send, sum2_recv):
    gx, gy, gz = sizes
    ix, iy, iz = lax.axis_index("gx"), lax.axis_index("gy"), lax.axis_index("gz")
    ox = 1 - ix
    base = 8
    inner = pl.ds(base, nz)
    above = pl.ds(base + 1, nz)
    below = pl.ds(base - 1, nz)
    half = nz // 2

    loads = [
        pltpu.make_async_copy(c_hbm, cond.at[pl.ds(1, nx), inner, :], load_sem.at[0]),
        pltpu.make_async_copy(a_hbm, absorb, load_sem.at[1]),
        pltpu.make_async_copy(r_hbm, rout, load_sem.at[2]),
    ]
    for load in loads:
        load.start()

    zero_slab = jnp.zeros((nz, LANES), F32)

    def clear(k, _):
        field[k, 0, inner, :] = zero_slab
        field[k, nx + 1, inner, :] = zero_slab
        return 0

    lax.fori_loop(0, 2 * STEPS + 2, clear, 0)
    cond[0, inner, :] = zero_slab
    cond[nx + 1, inner, :] = zero_slab
    zero_face = jnp.zeros((nx, LANES), F32)

    def clear_faces(k, _):
        for side in range(2):
            zrecv[k, side] = zero_face
            yrecv[k, side] = zero_face
        return 0

    lax.fori_loop(0, 2 * STEPS + 1, clear_faces, 0)

    barrier = pltpu.get_barrier_semaphore()
    group = [((ix + dx) % gx, (iy + dy) % gy) for dx in range(gx) for dy in range(gy) if (dx, dy) != (0, 0)]
    line = [(iz + d) % gz for d in range(1, gz)]
    for px, py in group:
        pl.semaphore_signal(barrier, inc=1, device_id=(px, py, iz), device_id_type=MESH)
    for pz in line:
        pl.semaphore_signal(barrier, inc=1, device_id=(ix, iy, pz), device_id_type=MESH)
    pl.semaphore_wait(barrier, len(group) + len(line))

    lane = lax.broadcasted_iota(jnp.int32, (half, LANES), 1)
    pair = lane // 2
    even = (lane % 2) == 0

    def pack(ref):
        out = jnp.zeros((half, LANES), F32)
        for x in range(nx):
            for h in range(2):
                v = ref[x + 1, pl.ds(base + half * h, half), :]
                out = jnp.where(pair == x + nx * h, pltpu.roll(v, (2 * x + 2 * nx * h + 1) % LANES, 1), out)
        return out

    def copies(ref, e):
        xc = pltpu.make_async_remote_copy(
            ref.at[jnp.where(ix == 0, nx, 1), inner, :], ref.at[jnp.where(ix == 0, 0, nx + 1), inner, :],
            face_send.at[e, 0], face_recv.at[e, 0], device_id=(ox, iy, iz), device_id_type=MESH)
        yc, zc = [], []
        for up in range(2):
            yc.append(pltpu.make_async_remote_copy(
                ysend.at[e], yrecv.at[e, 1 - up], face_send.at[e, 1 + up], face_recv.at[e, 2 - up],
                device_id=(ix, jnp.clip(iy + 2 * up - 1, 0, gy - 1), iz), device_id_type=MESH))
            zc.append(pltpu.make_async_remote_copy(
                zsend.at[e, up], zrecv.at[e, 1 - up], face_send.at[e, 3 + up], face_recv.at[e, 4 - up],
                device_id=(ix, iy, jnp.clip(iz + 2 * up - 1, 0, gz - 1)), device_id_type=MESH))
        return xc, yc, zc

    def send(ref, e):
        xc, yc, zc = copies(ref, e)
        xc.start()
        zsend[e, 0] = ref[pl.ds(1, nx), base, :]
        zsend[e, 1] = ref[pl.ds(1, nx), base + nz - 1, :]
        pl.when(iz > 0)(zc[0].start)
        pl.when(iz < gz - 1)(zc[1].start)
        ysend[e] = pack(ref)
        pl.when(iy > 0)(yc[0].start)
        pl.when(iy < gy - 1)(yc[1].start)

    def receive(ref, e):
        xc, yc, zc = copies(ref, e)
        xc.wait()
        pl.when(iy > 0)(lambda: (yc[0].wait_send(), yc[1].wait_recv())[0])
        pl.when(iy < gy - 1)(lambda: (yc[1].wait_send(), yc[0].wait_recv())[0])
        pl.when(iz > 0)(lambda: (zc[0].wait_send(), zc[1].wait_recv())[0])
        pl.when(iz < gz - 1)(lambda: (zc[1].wait_send(), zc[0].wait_recv())[0])
        ref[pl.ds(1, nx), base - 1, :] = zrecv[e, 0]
        ref[pl.ds(1, nx), base + nz, :] = zrecv[e, 1]
        both = jnp.where(even, yrecv[e, 0], pltpu.roll(yrecv[e, 1], LANES - 2, 1))
        for x in range(nx):
            for h in range(2):
                halo[x, pl.ds(half * h, half), :] = pltpu.roll(both, (LANES - 2 * x - 2 * nx * h) % LANES, 1)

    wide_lane = lax.broadcasted_iota(jnp.int32, (nz, LANES), 1)
    inside = wide_lane < LANES - 1
    edge = (wide_lane == 0) | (wide_lane == LANES - 1)

    loads[0].wait()
    send(cond, 0)
    loads[1].wait()
    loads[2].wait()
    receive(cond, 0)
    fx[0] = 0.5 * (cond[0, inner, :] + cond[1, inner, :])

    def coefficients(x, _):
        here = cond[x + 1, inner, :]
        xp = 0.5 * (here + cond[x + 2, inner, :])
        xm = fx[x]
        yp = jnp.where(inside, 0.5 * (here + pltpu.roll(here, LANES - 1, 1)), 0.0)
        ye = jnp.where(edge, 0.5 * (here + halo[x]), 0.0)
        zp = 0.5 * (here + cond[x + 1, above, :])
        zm = 0.5 * (here + cond[x + 1, below, :])
        total = absorb[x] + xp + xm + yp + pltpu.roll(yp, 1, 1) + ye + zp + zm
        inverse = 1.0 / total
        fx[x + 1] = xp
        fy[x] = yp
        ey[x] = ye
        fz[x, below, :] = zm
        fz[x, inner, :] = zp
        diag[x] = total
        weight[x] = (2.0 / RHO) * inverse
        field[0, x + 1, inner, :] = rout[x] * inverse
        return 0

    lax.fori_loop(0, nx, coefficients, 0)

    tiles = nz // 8

    def chain(first, exchange):
        def step(k, sums):
            src, dst, old = first + k, first + k + 1, jnp.maximum(first + k - 1, first)
            send(field.at[src], exchange + k)
            receive(field.at[src], exchange + k)
            scale = jnp.where(k == 0, 0.5, 1.0).astype(F32)
            keep = jnp.where(k == 0, 0.0, 1.0).astype(F32)

            def row(x, acc):
                same, next_ = acc
                v = field[src, x + 1, inner, :]
                y = fy[x]
                s = fx[x + 1] * field[src, x + 2, inner, :] + fx[x] * field[src, x, inner, :]
                s = s + fz[x, inner, :] * field[src, x + 1, above, :] + fz[x, below, :] * field[src, x + 1, below, :]
                s = s + y * pltpu.roll(v, LANES - 1, 1) + pltpu.roll(y * v, 1, 1) + ey[x] * halo[x]
                new = scale * (weight[x] * s) - keep * field[old, x + 1, inner, :]
                field[dst, x + 1, inner, :] = new
                w = diag[x] * v
                return same + w * v, next_ + w * new

            zero = jnp.zeros((nz, LANES), F32)
            same, next_ = lax.fori_loop(0, nx, row, (zero, zero), unroll=4)
            coef[2 * k] = jnp.sum(same.reshape(tiles, 8, LANES), axis=0)
            coef[2 * k + 1] = jnp.sum(next_.reshape(tiles, 8, LANES), axis=0)
            return sums

        lax.fori_loop(0, STEPS, step, 0)

    row_lane = lax.broadcasted_iota(jnp.int32, (1, LANES), 1)
    gxy = ix * gy + iy

    def total_of(n, which):
        out = jnp.zeros((1, LANES), F32)
        for m in range(n):
            one_row = jnp.sum(coef[m], axis=0, keepdims=True)
            out = jnp.where(row_lane == m, jnp.sum(one_row, axis=1, keepdims=True), out)
        for part, peers, mine, send_sem, recv_sem, where in (
            (part1, [(px, py, iz) for px, py in group], gxy, sum1_send, sum1_recv, [px * gy + py for px, py in group]),
            (part2, [(ix, iy, pz) for pz in line], iz, sum2_send, sum2_recv, line),
        ):
            part[which, mine] = out
            sent = []
            for i, peer in enumerate(peers):
                copy = pltpu.make_async_remote_copy(
                    part.at[which, mine], part.at[which, mine], send_sem.at[which, i], recv_sem.at[which, mine],
                    device_id=peer, device_id_type=MESH)
                copy.start()
                sent.append(copy)
            for i, slot in enumerate(where):
                pltpu.make_async_remote_copy(
                    part.at[which, slot], part.at[which, slot], send_sem.at[which, i], recv_sem.at[which, slot],
                    device_id=peers[i], device_id_type=MESH).wait_recv()
            for copy in sent:
                copy.wait_send()
            out = jnp.sum(part[which], axis=0)
        values = []
        for m in range(n):
            values.append(jnp.broadcast_to(jnp.sum(jnp.where(row_lane == m, out, 0.0), axis=1, keepdims=True), (8, LANES)))
        return values

    def moments(dots):
        mu = list(dots[:2])
        for m in range(2, len(dots)):
            mu.append(2.0 * dots[m] - mu[m % 2])
        return mu

    one = jnp.ones((8, LANES), F32)

    chain(0, 1)

    def last_dot(x, acc):
        v = field[STEPS, x + 1, inner, :]
        return acc + diag[x] * v * v

    acc = lax.fori_loop(0, nx, last_dot, jnp.zeros((nz, LANES), F32), unroll=4)
    coef[2 * STEPS] = jnp.sum(acc.reshape(tiles, 8, LANES), axis=0)
    mu = moments(total_of(2 * STEPS + 1, 0))
    x5, p5, q4, rho4 = first_block(mu, one)

    def spread(c):
        return jnp.broadcast_to(c[None], (tiles, 8, LANES)).reshape(nz, LANES)

    for k in range(STEPS + 1):
        coef[16 + k] = p5[k]

    def restart(x, _):
        acc = spread(coef[16]) * field[0, x + 1, inner, :]
        for k in range(1, STEPS + 1):
            acc = acc + spread(coef[16 + k]) * field[k, x + 1, inner, :]
        field[STEPS + 1, x + 1, inner, :] = acc
        return 0

    lax.fori_loop(0, nx, restart, 0, unroll=2)

    chain(STEPS + 1, STEPS + 1)
    nu = moments(total_of(2 * STEPS, 1))
    xs, ps = second_block(nu, p5, x5, q4, rho4, mu, one)
    names = [("t", k) for k in range(STEPS)] + [("y", k) for k in range(STEPS + 1)]
    where = list(range(STEPS)) + list(range(STEPS + 1, 2 * STEPS + 2))
    xs_at, ps_at = [], []
    slot = 16
    for name in names:
        for table, at in ((xs, xs_at), (ps, ps_at)):
            if name in table:
                coef[slot] = table[name]
                at.append(slot)
                slot += 1
            else:
                at.append(None)

    def finish(x, _):
        sx = sp = None
        for n, f in enumerate(where):
            v = field[f, x + 1, inner, :]
            if xs_at[n] is not None:
                t = spread(coef[xs_at[n]]) * v
                sx = t if sx is None else sx + t
            if ps_at[n] is not None:
                t = spread(coef[ps_at[n]]) * v
                sp = t if sp is None else sp + t
        xout[x] = sx
        rout[x] = diag[x] * sp
        return 0

    lax.fori_loop(0, nx, finish, 0)
    stores = [
        pltpu.make_async_copy(xout, x_hbm, store_sem.at[0]),
        pltpu.make_async_copy(rout, o_hbm, store_sem.at[1]),
    ]
    for store in stores:
        store.start()
    for store in stores:
        store.wait()


def solution(mesh):
    gx, gy, gz = mesh.shape["gx"], mesh.shape["gy"], mesh.shape["gz"]

    def on_device(right_side, conductivity, absorption):
        nx, ny, nz = right_side.shape
        assert ny == LANES and nx * 2 * 2 == LANES and gx == 2
        args = [jnp.transpose(v, (0, 2, 1)) for v in (right_side, conductivity, absorption)]
        block = (nx, nz, LANES)
        exchanges = 2 * STEPS + 1
        dma = pltpu.SemaphoreType.DMA
        tall = nz + 16
        out = pl.pallas_call(
            functools.partial(kernel, nx, nz, (gx, gy, gz)),
            out_shape=[jax.ShapeDtypeStruct(block, F32)] * 2,
            in_specs=[pl.BlockSpec(memory_space=pl.ANY)] * 3,
            out_specs=[pl.BlockSpec(memory_space=pl.ANY)] * 2,
            scratch_shapes=[
                pltpu.VMEM((nx + 2, tall, LANES), F32),
                pltpu.VMEM(block, F32),
                pltpu.VMEM(block, F32),
                pltpu.VMEM(block, F32),
                pltpu.VMEM((nx + 1, nz, LANES), F32),
                pltpu.VMEM(block, F32),
                pltpu.VMEM((nx, tall, LANES), F32),
                pltpu.VMEM(block, F32),
                pltpu.VMEM(block, F32),
                pltpu.VMEM((2 * STEPS + 2, nx + 2, tall, LANES), F32),
                pltpu.VMEM((exchanges, 2, nx, LANES), F32),
                pltpu.VMEM((exchanges, 2, nx, LANES), F32),
                pltpu.VMEM((exchanges, nz // 2, LANES), F32),
                pltpu.VMEM((exchanges, 2, nz // 2, LANES), F32),
                pltpu.VMEM((2, gx * gy, 1, LANES), F32),
                pltpu.VMEM((2, gz, 1, LANES), F32),
                pltpu.VMEM((48, 8, LANES), F32),
                pltpu.VMEM(block, F32),
                pltpu.VMEM(block, F32),
                dma((3,)),
                dma((2,)),
                dma((exchanges, 5)),
                dma((exchanges, 5)),
                dma((2, gx * gy)),
                dma((2, gx * gy)),
                dma((2, gz)),
                dma((2, gz)),
            ],
            compiler_params=pltpu.CompilerParams(
                collective_id=0, has_side_effects=True, vmem_limit_bytes=60 * 1024 * 1024
            ),
        )(*args)
        return tuple(jnp.transpose(v, (0, 2, 1)) for v in out)

    spec = P("gx", "gy", "gz")
    return jax.shard_map(on_device, mesh=mesh, in_specs=(spec,) * 3, out_specs=(spec,) * 2, check_vma=False)
```

time: 803 us -> 98.1 us (0.12); the launches traced: 791 us -> 97.1 us
  blocking collectives: 341 us -> 0 us
  other arithmetic: 143 us -> 0 us
  starting transfers between devices: 136 us -> 0 us
  local copies, waits for them, and re-layouts: 126 us -> 3.37 us
  Pallas kernels: 0 us -> 93 us
  between operations: 39.1 us -> 0.65 us
    psum x40 -> x0, blocking collectives: 341 us -> none  [over_axes(): return functools.reduce(lax.psum, axes, shard)]
    ppermute x66 -> x0, starting transfers between devices: 136 us -> none  [the longest x33 68.5 us: padded_2(): lax.ppermute(leading, axis, [(b, a) for a, b in up])]
    reduce_sum x10 -> x0, other arithmetic: 97.7 us -> none  [paired_dots(): jnp.sum(precond * image)]
    pallas_call x0 -> x1, Pallas kernels: none -> 93 us  [on_device(): pl.pallas_call(functools.partial(kernel, nx, nz, (gx, gy, gz)), out_shape...]
    slice x53 -> x0, local copies, waits for them, and re-layouts: 51.7 us -> none  [the longest x32 34.8 us: padded_2(): last = lax.slice_in_dim(shard, length - width, length, axis=dim)]
    pad x22 -> x0, local copies, waits for them, and re-layouts: 39 us -> none  [the longest x11 24.1 us: padded_2(): jnp.pad(low, around)]
    div x10 -> x0, other arithmetic: 33.9 us -> none  [on_device(): precond = residual / total]
    ppermute x22 -> x0, local copies, waits for them, and re-layouts: 29 us -> none  [the longest x11 14.5 us: padded_2(): lax.ppermute(last, axis, up)]
  transfers between devices with their start and end apart: 66 -> 0, of which waited for: 11 -> 0; matrix products, arithmetic and copies ran while one was open for 13% -> 0% of each run, Pallas kernels for 0% -> 0%
where the time goes in v1:
time: 98.1 us; the launch traced here: 97.1 us
  Pallas kernels  93 us (95%)
  local copies, waits for them, and re-layouts  3.37 us (3%)
    pallas_call x1, Pallas kernels, on_device(): pl.pallas_call(functools.partial(kernel, nx, nz, (gx, gy, gz)), out_shape...  93 us
    unnamed x4, local copies, waits for them, and re-layouts  3.37 us

profile of v1, /device:TPU:8, one launch (start us, length us, event | category | flops | bytes accessed | tf_op | source)
XLA Modules:
  0.0 97.1 jit_solution(8443799598792760222)
XLA Ops:
  0.6 93.0 %shard_map.50 = (f32[32,64,128]{2,1,0:T(8,128)}, f32[32,64,128]{2,1,0:T(8,128)}) custom-call(f32[32,64,128]{2,1,0:T(8,128)} %bitcast.5, f32[32,64,128]{2,1,0:T(8,128)} %bitcast.6, f32[32,64,128]{2,1,0:T(8,128)} %bitcast.7), custom_call_target="tpu_custom_call" | custom-call | tf_op jit(solution)/shard_map/pallas_call | solution.py:422
  93.7 0.0 copy-start
  93.7 2.4 %copy.7 = f32[32,128,64]{1,2,0:T(8,128)} copy(f32[32,128,64]{1,2,0:T(8,128)} %bitcast.9) | data formatting | bytes 2097152
  96.1 0.0 copy-done
  96.1 1.0 copy.8
Async XLA Ops:
  93.7 2.4 %copy-start = (f32[32,64,128]{2,1,0:T(8,128)S(1)}, f32[32,64,128]{2,1,0:T(8,128)}, u32[]{:S(2)}) copy-start(f32[32,64,128]{2,1,0:T(8,128)} %get-tuple-element.5) | copy-start | bytes 3145732

commit v2 on v0

v2 whole, which is shorter than its diff:
```python
import functools

import jax
import jax.numpy as jnp
from jax import lax
from jax.experimental import pallas as pl
from jax.experimental.pallas import tpu as pltpu
from jax.sharding import PartitionSpec as P

F32 = jnp.float32
MESH = pl.DeviceIdType.MESH
STEPS = 10
LANES = 128
BASE = 8


def two_sum(a, b):
    s = a + b
    t = s - a
    return s, (a - (s - t)) + (b - t)


def renew(a, b):
    s = a + b
    return s, b - (s - a)


def halves(a):
    t = 4097.0 * a
    high = t - (t - a)
    return high, a - high


def two_product(a, b):
    p = a * b
    ah, al = halves(a)
    bh, bl = halves(b)
    return p, ((ah * bh - p) + ah * bl + al * bh) + al * bl


def dadd(a, b):
    s, e = two_sum(a[0], b[0])
    return renew(s, e + (a[1] + b[1]))


def dneg(a):
    return -a[0], -a[1]


def dmul(a, b):
    p, e = two_product(a[0], b[0])
    return renew(p, e + (a[0] * b[1] + a[1] * b[0]))


def dtimes(a, power):
    return power * a[0], power * a[1]


def ddiv(a, b):
    q = a[0] / b[0]
    p, e = two_product(q, b[0])
    rest = ((a[0] - p) - e) + (a[1] - q * b[1])
    return renew(q, rest / b[0])


def jacobi_matrix(mu):
    n = len(mu) // 2
    cur = [mu[0]] + [dtimes(mu[k], 2.0 ** (1 - k)) for k in range(1, 2 * n)]
    prev = None
    ratio = ddiv(cur[1], cur[0])
    alpha, beta = [ratio], [None]
    for k in range(1, n):
        new = [None] * (2 * n)
        minus_alpha = dneg(alpha[-1])
        minus_beta = None if k == 1 else dneg(beta[-1])
        for l in range(k, 2 * n - k):
            v = dadd(cur[l + 1], dmul(minus_alpha, cur[l]))
            if prev is not None:
                v = dadd(v, dmul(minus_beta, prev[l]))
            new[l] = dadd(v, dtimes(cur[l - 1], 0.5 if l == 1 else 0.25))
        later = ddiv(new[k + 1], new[k])
        alpha.append(dadd(later, dneg(ratio)))
        beta.append(ddiv(new[k], cur[k - 1]))
        prev, cur, ratio = cur, new, later
    return [a[0] for a in alpha], [None if b is None else b[0] for b in beta]


def solution_polynomials(alpha, beta, kappa, one):
    n = len(alpha)
    tau = 0.5 * kappa
    at = [one, tau - alpha[0]]
    for k in range(1, n):
        at.append((tau - alpha[k]) * at[-1] - beta[k] * at[-2])
    before, p = None, [one]
    for k in range(n):
        new = [None] * (k + 2)

        def put(i, v):
            new[i] = v if new[i] is None else new[i] + v

        for i, v in enumerate(p):
            half = 0.5 * v
            put(i + 1, half)
            put(abs(i - 1), half)
        for i, v in enumerate(p):
            put(i, -(alpha[k] * v))
        if before is not None:
            for i, v in enumerate(before):
                put(i, -(beta[k] * v))
        before, p = p, new
    scale = one / at[n]
    residual = [scale * v for v in p]
    rest = [-v for v in residual]
    rest[0] = rest[0] + one
    q = [None] * (n + 2)
    zero = 0.0 * one
    q[n] = q[n + 1] = zero
    for k in range(n, 1, -1):
        q[k - 1] = (q[k] - rest[k]) * kappa - q[k + 1]
    q[0] = (q[1] - rest[1]) * tau - 0.5 * q[2]
    return q[:n], residual


def kernel(nx, nz, sizes, r_hbm, c_hbm, a_hbm, x_out, r_out,
           cond, absorb, diag, weight, fx, fy, fz, ey, turned, wx, wz, field, zsend, zrecv, ysend, yrecv, xrecv,
           part1, part2, dots, table, coef,
           load_sem, face_send, face_recv, sum1_send, sum1_recv, sum2_send, sum2_recv):
    gx, gy, gz = sizes
    ix, iy, iz = lax.axis_index("gx"), lax.axis_index("gy"), lax.axis_index("gz")
    ox = 1 - ix
    base = BASE
    inner = pl.ds(base, nz)
    above = pl.ds(base + 1, nz)
    below = pl.ds(base - 1, nz)
    half = nz // 2
    tiles = nz // 8
    low_x = ix == 0
    border = jnp.where(low_x, nx, 1)

    loads = [
        pltpu.make_async_copy(c_hbm, cond.at[pl.ds(1, nx), inner, :], load_sem.at[0]),
        pltpu.make_async_copy(a_hbm, absorb, load_sem.at[1]),
        pltpu.make_async_copy(r_hbm, r_out, load_sem.at[2]),
    ]
    for load in loads:
        load.start()

    zero_face = jnp.zeros((nx, LANES), F32)
    zero_slab = jnp.zeros((nz, LANES), F32)

    def clear_faces(k, _):
        for side in range(2):
            zrecv[k, side] = zero_face
            yrecv[k, side] = zero_face
        return 0

    lax.fori_loop(0, STEPS + 1, clear_faces, 0)

    barrier = pltpu.get_barrier_semaphore()
    group = [((ix + dx) % gx, (iy + dy) % gy) for dx in range(gx) for dy in range(gy) if (dx, dy) != (0, 0)]
    line = [(iz + d) % gz for d in range(1, gz)]
    for px, py in group:
        pl.semaphore_signal(barrier, inc=1, device_id=(px, py, iz), device_id_type=MESH)
    for pz in line:
        pl.semaphore_signal(barrier, inc=1, device_id=(ix, iy, pz), device_id_type=MESH)

    lane = lax.broadcasted_iota(jnp.int32, (half, LANES), 1)
    pair = lane // 2
    even = (lane % 2) == 0
    row_lane = lax.broadcasted_iota(jnp.int32, (1, LANES), 1)

    def tile_sum(v):
        return jnp.sum(v.reshape(tiles, 8, LANES), axis=0)

    def spread(c, rows=nz):
        return jnp.broadcast_to(c[None], (rows // 8, 8, LANES)).reshape(rows, LANES)

    def turn_of(x, h):
        return 2 * x + 2 * nx * h

    def pack(source):
        out = jnp.zeros((half, LANES), F32)
        for x in range(nx):
            for h in range(2):
                v = source[x + 1, pl.ds(base + half * h, half), :]
                out = jnp.where(pair == x + nx * h, pltpu.roll(v, (turn_of(x, h) + 1) % LANES, 1), out)
        return out

    def copies(source, e):
        xc = pltpu.make_async_remote_copy(
            source.at[border, inner, :], xrecv.at[e],
            face_send.at[e, 0], face_recv.at[e, 0], device_id=(ox, iy, iz), device_id_type=MESH)
        yc, zc = [], []
        for up in range(2):
            yc.append(pltpu.make_async_remote_copy(
                ysend.at[e], yrecv.at[e, 1 - up], face_send.at[e, 1 + up], face_recv.at[e, 2 - up],
                device_id=(ix, jnp.clip(iy + 2 * up - 1, 0, gy - 1), iz), device_id_type=MESH))
            zc.append(pltpu.make_async_remote_copy(
                zsend.at[e, up], zrecv.at[e, 1 - up], face_send.at[e, 3 + up], face_recv.at[e, 4 - up],
                device_id=(ix, iy, jnp.clip(iz + 2 * up - 1, 0, gz - 1)), device_id_type=MESH))
        return xc, yc, zc

    def send(source, e, packed):
        xc, yc, zc = copies(source, e)
        ysend[e] = packed
        zsend[e, 0] = source[pl.ds(1, nx), base, :]
        zsend[e, 1] = source[pl.ds(1, nx), base + nz - 1, :]
        pl.when(iz > 0)(zc[0].start)
        pl.when(iz < gz - 1)(zc[1].start)
        pl.when(iy > 0)(yc[0].start)
        pl.when(iy < gy - 1)(yc[1].start)
        xc.start()

    def receive(source, e):
        xc, yc, zc = copies(source, e)
        xc.wait()
        pl.when(iy > 0)(lambda: (yc[0].wait_send(), yc[1].wait_recv())[0])
        pl.when(iy < gy - 1)(lambda: (yc[1].wait_send(), yc[0].wait_recv())[0])
        pl.when(iz > 0)(lambda: (zc[0].wait_send(), zc[1].wait_recv())[0])
        pl.when(iz < gz - 1)(lambda: (zc[1].wait_send(), zc[0].wait_recv())[0])

    def beside(e):
        return jnp.where(even, yrecv[e, 0], pltpu.roll(yrecv[e, 1], LANES - 2, 1))

    gxy = ix * gy + iy
    first = (part1, [(px, py, iz) for px, py in group], gxy, sum1_send, sum1_recv, [px * gy + py for px, py in group])
    second = (part2, [(ix, iy, pz) for pz in line], iz, sum2_send, sum2_recv, line)

    def spread_out(stage, which):
        part, peers, mine, send_sem, recv_sem, _ = stage
        for i, peer in enumerate(peers):
            pltpu.make_async_remote_copy(
                part.at[which, mine], part.at[which, mine], send_sem.at[which, i], recv_sem.at[which, mine],
                device_id=peer, device_id_type=MESH).start()

    def gather_in(stage, which):
        part, peers, _, send_sem, recv_sem, slots = stage
        for i, slot in enumerate(slots):
            copy = pltpu.make_async_remote_copy(
                part.at[which, slot], part.at[which, slot], send_sem.at[which, i], recv_sem.at[which, slot],
                device_id=peers[i], device_id_type=MESH)
            copy.wait_recv()
            copy.wait_send()
        total, error = part[which, 0], jnp.zeros_like(part[which, 0])
        for i in range(1, part.shape[1]):
            total, e = two_sum(total, part[which, i])
            error = error + e
        return total, error

    def sum_begin(which, row):
        part1[which, gxy] = row
        spread_out(first, which)

    def sum_middle(which):
        high, low = renew(*gather_in(first, which))
        part2[which, iz, pl.ds(0, 1), :] = high
        part2[which, iz, pl.ds(1, 1), :] = low
        spread_out(second, which)

    def sum_end(which):
        total, error = gather_in(second, which)
        return renew(total[0:1], error[0:1] + total[1:2])

    def all_lanes(row, m):
        return jnp.broadcast_to(jnp.sum(jnp.where(row_lane == m, row, 0.0), axis=1, keepdims=True), (8, LANES))

    def one_row(values):
        row = jnp.zeros((1, LANES), F32)
        for m, v in enumerate(values):
            row = jnp.where(row_lane == m, jnp.sum(jnp.sum(v, axis=0, keepdims=True), axis=1, keepdims=True), row)
        return row

    wide_lane = lax.broadcasted_iota(jnp.int32, (nz, LANES), 1)
    inside = wide_lane < LANES - 1
    edge = (wide_lane == 0) | (wide_lane == LANES - 1)
    one = jnp.ones((8, LANES), F32)

    loads[0].wait()
    packed = pack(cond)
    pl.semaphore_wait(barrier, len(group) + len(line))
    send(cond, 0, packed)
    loads[1].wait()

    def means(x, acc):
        return acc[0] + cond[x + 1, inner, :], acc[1] + absorb[x]

    sums = lax.fori_loop(0, nx, means, (zero_slab, zero_slab), unroll=4)
    sum_begin(0, one_row([tile_sum(v) for v in sums]))

    def clear(k, _):
        field[k, 0, inner, :] = zero_slab
        field[k, nx + 1, inner, :] = zero_slab
        field[k, pl.ds(1, nx), base - 1, :] = zero_face
        field[k, pl.ds(1, nx), base + nz, :] = zero_face
        return 0

    lax.fori_loop(0, STEPS, clear, 0)
    table[0, 0] = one
    table[0, 1] = jnp.zeros((8, LANES), F32)
    loads[2].wait()
    receive(cond, 0)
    sum_middle(0)

    cond[jnp.where(low_x, nx + 1, 0), inner, :] = xrecv[0]
    cond[jnp.where(low_x, 0, nx + 1), inner, :] = zero_slab
    cond[pl.ds(1, nx), base - 1, :] = zrecv[0, 0]
    cond[pl.ds(1, nx), base + nz, :] = zrecv[0, 1]
    for_c = beside(0)
    for x in range(nx):
        for h in range(2):
            ey[x, pl.ds(half * h, half), :] = pltpu.roll(for_c, (LANES - turn_of(x, h)) % LANES, 1)
    fx[0] = 0.5 * (cond[0, inner, :] + cond[1, inner, :])

    def coefficients(x, _):
        here = cond[x + 1, inner, :]
        xp = 0.5 * (here + cond[x + 2, inner, :])
        xm = fx[x]
        yp = jnp.where(inside, 0.5 * (here + pltpu.roll(here, LANES - 1, 1)), 0.0)
        ye = jnp.where(edge, 0.5 * (here + ey[x]), 0.0)
        zp = 0.5 * (here + cond[x + 1, above, :])
        zm = 0.5 * (here + cond[x + 1, below, :])
        total = absorb[x] + xp + xm + yp + pltpu.roll(yp, 1, 1) + ye + zp + zm
        inverse = 1.0 / total
        fx[x + 1] = xp
        fy[x] = yp
        ey[x] = ye * inverse
        fz[x, below, :] = zm
        fz[x, inner, :] = zp
        diag[x] = total
        weight[x] = inverse
        field[0, x + 1, inner, :] = r_out[x] * inverse
        return 0

    lax.fori_loop(0, nx, coefficients, 0, unroll=2)
    wx[...] = weight[border - 1] * fx[jnp.where(low_x, nx, 0)]
    wz[0] = weight[pl.ds(0, nx), 0, :] * fz[pl.ds(0, nx), base - 1, :]
    wz[1] = weight[pl.ds(0, nx), nz - 1, :] * fz[pl.ds(0, nx), base + nz - 1, :]

    send(field.at[0], 1, pack(field.at[0]))

    def step(k, _):
        src, dst, old = k, k + 1, jnp.maximum(k - 1, 0)
        e = k + 1

        @pl.when(k == 1)
        def _():
            high, _ = sum_end(0)
            six = 6.0 * all_lanes(high, 0)
            rho = 0.97 * six / (six + all_lanes(high, 1))
            kappa = jnp.floor(64.0 * (2.0 / rho)) * (1.0 / 64.0)
            half_kappa = 0.5 * kappa
            table[1, 0] = kappa * half_kappa
            table[1, 1] = one
            table[2, 0] = kappa
            table[2, 1] = half_kappa
            for j in range(3, STEPS):
                table[j, 0] = kappa
                table[j, 1] = one

        a = table[k, 0]
        a_all, b_all = spread(a), spread(table[k, 1])

        def row(x, acc):
            same, older = acc
            v = field[src, x + 1, inner, :]
            y = fy[x]
            o = field[old, x + 1, inner, :]
            s = fx[x + 1] * field[src, x + 2, inner, :] + fx[x] * field[src, x, inner, :]
            s = s + fz[x, inner, :] * field[src, x + 1, above, :] + fz[x, below, :] * field[src, x + 1, below, :]
            s = s + y * pltpu.roll(v, LANES - 1, 1) + pltpu.roll(y * v, 1, 1)
            field[dst, x + 1, inner, :] = a_all * (weight[x] * s) - b_all * o
            w = diag[x] * v
            return same + w * v, older + w * o

        same, older = lax.fori_loop(0, nx, row, (zero_slab, zero_slab), unroll=4)
        dots[2 * k] = tile_sum(same)
        dots[2 * k + 1] = tile_sum(older)

        receive(field.at[src], e)
        a_half = spread(a, half)
        field[dst, pl.ds(1, nx), base, :] += a_half * wz[0] * zrecv[e, 0]
        field[dst, pl.ds(1, nx), base + nz - 1, :] += a_half * wz[1] * zrecv[e, 1]
        field[dst, border, inner, :] += a_all * wx[...] * xrecv[e]
        sides = a_half * beside(e)
        for x in range(nx):
            for h in range(2):
                turned[x, pl.ds(half * h, half), :] = pltpu.roll(sides, (LANES - turn_of(x, h)) % LANES, 1)

        def add_sides(x, _):
            field[dst, x + 1, inner, :] += ey[x] * turned[x]
            return 0

        lax.fori_loop(0, nx, add_sides, 0, unroll=4)
        packed = pack(field.at[dst])

        @pl.when(k < STEPS - 1)
        def _():
            send(field.at[dst], e + 1, packed)

        return 0

    lax.fori_loop(0, STEPS, step, 0)

    def last_dot(x, acc):
        return acc + diag[x] * field[STEPS, x + 1, inner, :] * field[STEPS - 1, x + 1, inner, :]

    dots[2 * STEPS + 1] = tile_sum(lax.fori_loop(0, nx, last_dot, zero_slab, unroll=4))
    sum_begin(1, one_row([dots[m if m % 2 == 0 else m + 2] for m in range(2 * STEPS)]))
    sum_middle(1)
    high, low = sum_end(1)
    kappa = table[2, 0]
    half_kappa = table[2, 1]
    raw = [(all_lanes(high, m), all_lanes(low, m)) for m in range(2 * STEPS)]
    exact = (half_kappa, jnp.zeros((8, LANES), F32))
    raw[1] = dmul(raw[1], exact)
    raw[2] = dmul(dmul(raw[2], exact), exact)
    raw[3] = dmul(raw[3], exact)
    mu = raw[:2]
    for m in range(2, 2 * STEPS):
        mu.append(dadd(dtimes(raw[m], 2.0), dneg(mu[m % 2])))
    alpha, beta = jacobi_matrix(mu)
    xs, rs = solution_polynomials(alpha, beta, kappa, one)
    xs[1] = xs[1] * half_kappa
    rs[1] = rs[1] * half_kappa
    for k, v in enumerate(xs):
        coef[k] = v
    for k, v in enumerate(rs):
        coef[16 + k] = v

    def finish(x, _):
        v = field[0, x + 1, inner, :]
        sx = spread(coef[0]) * v
        sr = spread(coef[16]) * v
        for k in range(1, STEPS + 1):
            v = field[k, x + 1, inner, :]
            if k < STEPS:
                sx = sx + spread(coef[k]) * v
            sr = sr + spread(coef[16 + k]) * v
        x_out[x] = sx
        r_out[x] = diag[x] * sr
        return 0

    lax.fori_loop(0, nx, finish, 0)


def solution(mesh):
    gx, gy, gz = mesh.shape["gx"], mesh.shape["gy"], mesh.shape["gz"]

    def on_device(right_side, conductivity, absorption):
        nx, ny, nz = right_side.shape
        assert ny == LANES and nx * 2 * 2 == LANES and gx == 2
        args = [jnp.transpose(v, (0, 2, 1)) for v in (right_side, conductivity, absorption)]
        block = (nx, nz, LANES)
        exchanges = STEPS + 1
        dma = pltpu.SemaphoreType.DMA
        tall = nz + 16
        out = pl.pallas_call(
            functools.partial(kernel, nx, nz, (gx, gy, gz)),
            out_shape=[jax.ShapeDtypeStruct(block, F32)] * 2,
            in_specs=[pl.BlockSpec(memory_space=pl.ANY)] * 3,
            out_specs=[pl.BlockSpec(memory_space=pltpu.VMEM)] * 2,
            scratch_shapes=[
                pltpu.VMEM((nx + 2, tall, LANES), F32),
                pltpu.VMEM(block, F32),
                pltpu.VMEM(block, F32),
                pltpu.VMEM(block, F32),
                pltpu.VMEM((nx + 1, nz, LANES), F32),
                pltpu.VMEM(block, F32),
                pltpu.VMEM((nx, tall, LANES), F32),
                pltpu.VMEM(block, F32),
                pltpu.VMEM(block, F32),
                pltpu.VMEM((nz, LANES), F32),
                pltpu.VMEM((2, nx, LANES), F32),
                pltpu.VMEM((STEPS + 1, nx + 2, tall, LANES), F32),
                pltpu.VMEM((exchanges, 2, nx, LANES), F32),
                pltpu.VMEM((exchanges, 2, nx, LANES), F32),
                pltpu.VMEM((exchanges, nz // 2, LANES), F32),
                pltpu.VMEM((exchanges, 2, nz // 2, LANES), F32),
                pltpu.VMEM((exchanges, nz, LANES), F32),
                pltpu.VMEM((2, gx * gy, 1, LANES), F32),
                pltpu.VMEM((2, gz, 2, LANES), F32),
                pltpu.VMEM((2 * STEPS + 2, 8, LANES), F32),
                pltpu.VMEM((STEPS, 2, 8, LANES), F32),
                pltpu.VMEM((32, 8, LANES), F32),
                dma((3,)),
                dma((exchanges, 5)),
                dma((exchanges, 5)),
                dma((2, gx * gy)),
                dma((2, gx * gy)),
                dma((2, gz)),
                dma((2, gz)),
            ],
            compiler_params=pltpu.CompilerParams(
                collective_id=0, has_side_effects=True, vmem_limit_bytes=48 * 1024 * 1024
            ),
        )(*[pltpu.with_memory_space_constraint(v, pltpu.HBM) for v in args])
        return tuple(jnp.transpose(v, (0, 2, 1)) for v in out)

    spec = P("gx", "gy", "gz")
    return jax.shard_map(on_device, mesh=mesh, in_specs=(spec,) * 3, out_specs=(spec,) * 2, check_vma=False)
```

time: 803 us -> 78.2 us (0.10); the launches traced: 791 us -> 77.2 us
  blocking collectives: 341 us -> 0 us
  other arithmetic: 143 us -> 0 us
  starting transfers between devices: 136 us -> 0 us
  local copies, waits for them, and re-layouts: 126 us -> 1.94 us
  Pallas kernels: 0 us -> 74.6 us
  between operations: 39.1 us -> 0.64 us
    psum x40 -> x0, blocking collectives: 341 us -> none  [over_axes(): return functools.reduce(lax.psum, axes, shard)]
    ppermute x66 -> x0, starting transfers between devices: 136 us -> none  [the longest x33 68.5 us: padded_2(): lax.ppermute(leading, axis, [(b, a) for a, b in up])]
    reduce_sum x10 -> x0, other arithmetic: 97.7 us -> none  [paired_dots(): jnp.sum(precond * image)]
    pallas_call x0 -> x1, Pallas kernels: none -> 74.6 us  [on_device(): pl.pallas_call(functools.partial(kernel, nx, nz, (gx, gy, gz)), out_shape...]
    slice x53 -> x0, local copies, waits for them, and re-layouts: 51.7 us -> none  [the longest x32 34.8 us: padded_2(): last = lax.slice_in_dim(shard, length - width, length, axis=dim)]
    pad x22 -> x0, local copies, waits for them, and re-layouts: 39 us -> none  [the longest x11 24.1 us: padded_2(): jnp.pad(low, around)]
    div x10 -> x0, other arithmetic: 33.9 us -> none  [on_device(): precond = residual / total]
    ppermute x22 -> x0, local copies, waits for them, and re-layouts: 29 us -> none  [the longest x11 14.5 us: padded_2(): lax.ppermute(last, axis, up)]
  transfers between devices with their start and end apart: 66 -> 0, of which waited for: 11 -> 0; matrix products, arithmetic and copies ran while one was open for 13% -> 0% of each run, Pallas kernels for 0% -> 0%
where the time goes in v2:
time: 78.2 us; the launch traced here: 77.2 us
  Pallas kernels  74.6 us (95%)
  local copies, waits for them, and re-layouts  1.94 us (2%)
    pallas_call x1, Pallas kernels, on_device(): pl.pallas_call(functools.partial(kernel, nx, nz, (gx, gy, gz)), out_shape...  74.6 us
    unnamed x2, local copies, waits for them, and re-layouts  1.94 us

profile of v2, /device:TPU:8, one launch (start us, length us, event | category | flops | bytes accessed | tf_op | source)
XLA Modules:
  0.0 77.2 jit_solution(16668727584829318243)
XLA Ops:
  0.6 74.6 %shard_map.50 = (f32[32,64,128]{2,1,0:T(8,128)S(1)}, f32[32,64,128]{2,1,0:T(8,128)S(1)}) custom-call(f32[32,64,128]{2,1,0:T(8,128)} %bitcast.7, f32[32,64,128]{2,1,0:T(8,128)} %bitcast.8, f32[32,64,128]{2,1,0:T(8,128)} %bitcast.9), custom_call_target="tpu_custom_call" | custom-call | tf_op jit(solution)/shard_map/pallas_call | solution.py:457
  75.2 1.0 %copy.7 = f32[32,128,64]{1,2,0:T(8,128)} copy(f32[32,128,64]{1,2,0:T(8,128)S(1)} %bitcast.6) | data formatting | bytes 2097152
  76.2 1.0 %copy.8 = f32[32,128,64]{1,2,0:T(8,128)} copy(f32[32,128,64]{1,2,0:T(8,128)S(1)} %bitcast.5) | data formatting | bytes 2097152

commit v3 on v2

--- a/solution.py
+++ b/solution.py
@@ -122,7 +122,7 @@
 
 
 def kernel(nx, nz, sizes, r_hbm, c_hbm, a_hbm, x_out, r_out,
-           cond, absorb, diag, weight, fx, fy, fz, ey, turned, wx, wz, field, zsend, zrecv, ysend, yrecv, xrecv,
+           cond, absorb, diag, weight, fx, fy, fz, turned, wx, wy, wz, xadd, yadd, zadd, field, xsend, zsend, zrecv, ysend, yrecv, xrecv,
            part1, part2, dots, table, coef,
            load_sem, face_send, face_recv, sum1_send, sum1_recv, sum2_send, sum2_recv):
     gx, gy, gz = sizes
@@ -186,9 +186,9 @@
                 out = jnp.where(pair == x + nx * h, pltpu.roll(v, (turn_of(x, h) + 1) % LANES, 1), out)
         return out
 
-    def copies(source, e):
+    def copies(e):
         xc = pltpu.make_async_remote_copy(
-            source.at[border, inner, :], xrecv.at[e],
+            xsend.at[e], xrecv.at[e],
             face_send.at[e, 0], face_recv.at[e, 0], device_id=(ox, iy, iz), device_id_type=MESH)
         yc, zc = [], []
         for up in range(2):
@@ -200,19 +200,23 @@
                 device_id=(ix, iy, jnp.clip(iz + 2 * up - 1, 0, gz - 1)), device_id_type=MESH))
         return xc, yc, zc
 
-    def send(source, e, packed):
-        xc, yc, zc = copies(source, e)
-        ysend[e] = packed
-        zsend[e, 0] = source[pl.ds(1, nx), base, :]
-        zsend[e, 1] = source[pl.ds(1, nx), base + nz - 1, :]
+    def send(e):
+        xc, yc, zc = copies(e)
         pl.when(iz > 0)(zc[0].start)
         pl.when(iz < gz - 1)(zc[1].start)
         pl.when(iy > 0)(yc[0].start)
         pl.when(iy < gy - 1)(yc[1].start)
         xc.start()
 
-    def receive(source, e):
-        xc, yc, zc = copies(source, e)
+    def send_field(source, e):
+        ysend[e] = pack(source)
+        zsend[e, 0] = source[pl.ds(1, nx), base, :]
+        zsend[e, 1] = source[pl.ds(1, nx), base + nz - 1, :]
+        xsend[e] = source[border, inner, :]
+        send(e)
+
+    def receive(e):
+        xc, yc, zc = copies(e)
         xc.wait()
         pl.when(iy > 0)(lambda: (yc[0].wait_send(), yc[1].wait_recv())[0])
         pl.when(iy < gy - 1)(lambda: (yc[1].wait_send(), yc[0].wait_recv())[0])
@@ -276,9 +280,8 @@
     one = jnp.ones((8, LANES), F32)
 
     loads[0].wait()
-    packed = pack(cond)
     pl.semaphore_wait(barrier, len(group) + len(line))
-    send(cond, 0, packed)
+    send_field(cond, 0)
     loads[1].wait()
 
     def means(x, acc):
@@ -298,7 +301,7 @@
     table[0, 0] = one
     table[0, 1] = jnp.zeros((8, LANES), F32)
     loads[2].wait()
-    receive(cond, 0)
+    receive(0)
     sum_middle(0)
 
     cond[jnp.where(low_x, nx + 1, 0), inner, :] = xrecv[0]
@@ -308,7 +311,7 @@
     for_c = beside(0)
     for x in range(nx):
         for h in range(2):
-            ey[x, pl.ds(half * h, half), :] = pltpu.roll(for_c, (LANES - turn_of(x, h)) % LANES, 1)
+            turned[x, pl.ds(half * h, half), :] = pltpu.roll(for_c, (LANES - turn_of(x, h)) % LANES, 1)
     fx[0] = 0.5 * (cond[0, inner, :] + cond[1, inner, :])
 
     def coefficients(x, _):
@@ -316,14 +319,14 @@
         xp = 0.5 * (here + cond[x + 2, inner, :])
         xm = fx[x]
         yp = jnp.where(inside, 0.5 * (here + pltpu.roll(here, LANES - 1, 1)), 0.0)
-        ye = jnp.where(edge, 0.5 * (here + ey[x]), 0.0)
+        ye = jnp.where(edge, 0.5 * (here + turned[x]), 0.0)
         zp = 0.5 * (here + cond[x + 1, above, :])
         zm = 0.5 * (here + cond[x + 1, below, :])
         total = absorb[x] + xp + xm + yp + pltpu.roll(yp, 1, 1) + ye + zp + zm
         inverse = 1.0 / total
         fx[x + 1] = xp
         fy[x] = yp
-        ey[x] = ye * inverse
+        turned[x] = ye * inverse
         fz[x, below, :] = zm
         fz[x, inner, :] = zp
         diag[x] = total
@@ -336,7 +339,37 @@
     wz[0] = weight[pl.ds(0, nx), 0, :] * fz[pl.ds(0, nx), base - 1, :]
     wz[1] = weight[pl.ds(0, nx), nz - 1, :] * fz[pl.ds(0, nx), base + nz - 1, :]
 
-    send(field.at[0], 1, pack(field.at[0]))
+    send_field(field.at[0], 1)
+    packed = jnp.zeros((half, LANES), F32)
+    for x in range(nx):
+        for h in range(2):
+            v = turned[x, pl.ds(half * h, half), :]
+            packed = jnp.where(pair == x + nx * h, pltpu.roll(v, (turn_of(x, h) + 1) % LANES, 1), packed)
+    wy[...] = packed
+    zadd[0] = zero_face
+    zadd[1] = zero_face
+    xadd[...] = zero_slab
+    yadd[...] = jnp.zeros((half, LANES), F32)
+
+    face_row = lax.broadcasted_iota(jnp.int32, (nx, LANES), 0)
+    face_lane = lax.broadcasted_iota(jnp.int32, (nx, LANES), 1)
+    half_row = lax.broadcasted_iota(jnp.int32, (half, LANES), 0)
+    slab_row = lax.broadcasted_iota(jnp.int32, (nz, LANES), 0)
+
+    def correct(k):
+        field[k, pl.ds(1, nx), base, :] += zadd[0]
+        field[k, pl.ds(1, nx), base + nz - 1, :] += zadd[1]
+        field[k, border, inner, :] += xadd[...]
+        terms = yadd[...]
+        for x in range(nx):
+            for h in range(2):
+                turned[x, pl.ds(half * h, half), :] = pltpu.roll(terms, (LANES - turn_of(x, h) - 1) % LANES, 1)
+
+        def add_sides(x, _):
+            field[k, x + 1, inner, :] += jnp.where(edge, turned[x], 0.0)
+            return 0
+
+        lax.fori_loop(0, nx, add_sides, 0, unroll=4)
 
     def step(k, _):
         src, dst, old = k, k + 1, jnp.maximum(k - 1, 0)
@@ -357,6 +390,7 @@
                 table[j, 0] = kappa
                 table[j, 1] = one
 
+        correct(k)
         a = table[k, 0]
         a_all, b_all = spread(a), spread(table[k, 1])
 
@@ -376,30 +410,53 @@
         dots[2 * k] = tile_sum(same)
         dots[2 * k + 1] = tile_sum(older)
 
-        receive(field.at[src], e)
+        ypart = pack(field.at[dst])
+        zpart = [field[dst, pl.ds(1, nx), base + row_, :] for row_ in (0, nz - 1)]
+        xpart = field[dst, border, inner, :]
+
+        receive(e)
         a_half = spread(a, half)
-        field[dst, pl.ds(1, nx), base, :] += a_half * wz[0] * zrecv[e, 0]
-        field[dst, pl.ds(1, nx), base + nz - 1, :] += a_half * wz[1] * zrecv[e, 1]
-        field[dst, border, inner, :] += a_all * wx[...] * xrecv[e]
-        sides = a_half * beside(e)
-        for x in range(nx):
-            for h in range(2):
-                turned[x, pl.ds(half * h, half), :] = pltpu.roll(sides, (LANES - turn_of(x, h)) % LANES, 1)
-
-        def add_sides(x, _):
-            field[dst, x + 1, inner, :] += ey[x] * turned[x]
-            return 0
-
-        lax.fori_loop(0, nx, add_sides, 0, unroll=4)
-        packed = pack(field.at[dst])
+        sides = jnp.where(even, pltpu.roll(yrecv[e, 1], LANES - 1, 1), pltpu.roll(yrecv[e, 0], 1, 1))
+        ya = a_half * wy[...] * sides
+        za = [a_half * wz[i] * zrecv[e, i] for i in range(2)]
+        xa = a_all * wx[...] * xrecv[e]
+        yadd[...] = ya
+        zadd[0] = za[0]
+        zadd[1] = za[1]
+        xadd[...] = xa
 
         @pl.when(k < STEPS - 1)
         def _():
-            send(field.at[dst], e + 1, packed)
+            yface, xface = ypart + ya, xpart + xa
+            xlanes = []
+            for h in range(2):
+                here = 2 * nx * h + 1
+                at = half_row == (nz - 1 - half) * h
+                moved = jnp.where(face_lane // 2 == face_row + nx * h, pltpu.roll(za[h], here, 1, stride=2, stride_axis=0), 0.0)
+                yface = yface + jnp.where(at, jnp.sum(moved, axis=0, keepdims=True), 0.0)
+                xa_half = xa[half * h:half * (h + 1)]
+                turns = [(2 * (nx - 1) + here) % LANES, here]
+                moved = jnp.where(low_x, pltpu.roll(xa_half, turns[0], 1), pltpu.roll(xa_half, turns[1], 1))
+                yface = yface + jnp.where(pair == border - 1 + nx * h, moved, 0.0)
+                moved = jnp.where(low_x, pltpu.roll(ya, (LANES - turns[0]) % LANES, 1), pltpu.roll(ya, LANES - turns[1], 1))
+                xlanes.append(moved)
+                line_ = jnp.sum(jnp.where(at, ya, 0.0), axis=0, keepdims=True)
+                zface = zpart[h] + za[h]
+                for at_lane, shift in ((LANES - 1, 0), (0, 1)):
+                    one_lane = jnp.where(face_lane == 2 * face_row + 2 * nx * h + shift, line_, 0.0)
+                    zface = zface + jnp.where(face_lane == at_lane, jnp.sum(one_lane, axis=1, keepdims=True), 0.0)
+                z_at = slab_row == (nz - 1) * h
+                zface = zface + jnp.where(face_row == border - 1, jnp.sum(jnp.where(z_at, xa, 0.0), axis=0, keepdims=True), 0.0)
+                zsend[e + 1, h] = zface
+                xface = xface + jnp.where(z_at, jnp.sum(jnp.where(face_row == border - 1, za[h], 0.0), axis=0, keepdims=True), 0.0)
+            xsend[e + 1] = xface + jnp.where(edge, jnp.concatenate(xlanes, axis=0), 0.0)
+            ysend[e + 1] = yface
+            send(e + 1)
 
         return 0
 
     lax.fori_loop(0, STEPS, step, 0)
+    correct(STEPS)
 
     def last_dot(x, acc):
         return acc + diag[x] * field[STEPS, x + 1, inner, :] * field[STEPS - 1, x + 1, inner, :]
@@ -468,10 +525,14 @@
                 pltpu.VMEM(block, F32),
                 pltpu.VMEM((nx, tall, LANES), F32),
                 pltpu.VMEM(block, F32),
-                pltpu.VMEM(block, F32),
                 pltpu.VMEM((nz, LANES), F32),
+                pltpu.VMEM((nz // 2, LANES), F32),
+                pltpu.VMEM((2, nx, LANES), F32),
+                pltpu.VMEM((nz, LANES), F32),
+                pltpu.VMEM((nz // 2, LANES), F32),
                 pltpu.VMEM((2, nx, LANES), F32),
                 pltpu.VMEM((STEPS + 1, nx + 2, tall, LANES), F32),
+                pltpu.VMEM((exchanges, nz, LANES), F32),
                 pltpu.VMEM((exchanges, 2, nx, LANES), F32),
                 pltpu.VMEM((exchanges, 2, nx, LANES), F32),
                 pltpu.VMEM((exchanges, nz // 2, LANES), F32),

time: 78.2 us -> 71.4 us (0.913)
  Pallas kernels: 74.6 us -> 67.8 us
    pallas_call x1, Pallas kernels: 74.6 us -> 67.8 us  [on_device(): pl.pallas_call(functools.partial(kernel, nx, nz, (gx, gy, gz)), out_shape...]
where the time goes in v3:
time: 71.4 us; the launch traced here: 70.3 us
  Pallas kernels  67.8 us (95%)
  local copies, waits for them, and re-layouts  1.94 us (3%)
    pallas_call x1, Pallas kernels, on_device(): pl.pallas_call(functools.partial(kernel, nx, nz, (gx, gy, gz)), out_shape...  67.8 us
    unnamed x2, local copies, waits for them, and re-layouts  1.94 us

profile of v3, /device:TPU:8, one launch (start us, length us, event | category | flops | bytes accessed | tf_op | source)
XLA Modules:
  0.0 70.3 jit_solution(16257027043973197704)
XLA Ops:
  0.6 67.8 %shard_map.50 = (f32[32,64,128]{2,1,0:T(8,128)S(1)}, f32[32,64,128]{2,1,0:T(8,128)S(1)}) custom-call(f32[32,64,128]{2,1,0:T(8,128)} %bitcast.7, f32[32,64,128]{2,1,0:T(8,128)} %bitcast.8, f32[32,64,128]{2,1,0:T(8,128)} %bitcast.9), custom_call_target="tpu_custom_call" | custom-call | tf_op jit(solution)/shard_map/pallas_call | solution.py:514
  68.4 1.0 %copy.7 = f32[32,128,64]{1,2,0:T(8,128)} copy(f32[32,128,64]{1,2,0:T(8,128)S(1)} %bitcast.6) | data formatting | bytes 2097152
  69.4 1.0 %copy.8 = f32[32,128,64]{1,2,0:T(8,128)} copy(f32[32,128,64]{1,2,0:T(8,128)S(1)} %bitcast.5) | data formatting | bytes 2097152

commit v4 on v3

--- a/solution.py
+++ b/solution.py
@@ -64,8 +64,9 @@
 
 
 def jacobi_matrix(mu):
-    n = len(mu) // 2
-    cur = [mu[0]] + [dtimes(mu[k], 2.0 ** (1 - k)) for k in range(1, 2 * n)]
+    n = (len(mu) + 1) // 2
+    zero = (0.0 * mu[0][0], 0.0 * mu[0][0])
+    cur = [mu[0]] + [dtimes(mu[k], 2.0 ** (1 - k)) for k in range(1, 2 * n - 1)] + [zero]
     prev = None
     ratio = ddiv(cur[1], cur[0])
     alpha, beta = [ratio], [None]
@@ -78,18 +79,31 @@
             if prev is not None:
                 v = dadd(v, dmul(minus_beta, prev[l]))
             new[l] = dadd(v, dtimes(cur[l - 1], 0.5 if l == 1 else 0.25))
-        later = ddiv(new[k + 1], new[k])
-        alpha.append(dadd(later, dneg(ratio)))
         beta.append(ddiv(new[k], cur[k - 1]))
-        prev, cur, ratio = cur, new, later
-    return [a[0] for a in alpha], [None if b is None else b[0] for b in beta]
+        prev, cur = cur, new
+        if k < n - 1:
+            later = ddiv(new[k + 1], new[k])
+            alpha.append(dadd(later, dneg(ratio)))
+            ratio = later
+    high = [a[0] for a in alpha], [None if b is None else b[0] for b in beta]
+    return high[0], high[1], cur[n], cur[n - 1], ratio
+
+
+def without_pole(p, kappa):
+    n = len(p) - 1
+    q = [None] * (n + 2)
+    q[n] = q[n + 1] = 0.0 * kappa
+    for k in range(n, 1, -1):
+        q[k - 1] = (q[k] + p[k]) * kappa - q[k + 1]
+    q[0] = (q[1] + p[1]) * (0.5 * kappa) - 0.5 * q[2]
+    return q[:n]
 
 
 def solution_polynomials(alpha, beta, kappa, one):
-    n = len(alpha)
+    n = len(beta)
     tau = 0.5 * kappa
     at = [one, tau - alpha[0]]
-    for k in range(1, n):
+    for k in range(1, n - 1):
         at.append((tau - alpha[k]) * at[-1] - beta[k] * at[-2])
     before, p = None, [one]
     for k in range(n):
@@ -102,27 +116,20 @@
             half = 0.5 * v
             put(i + 1, half)
             put(abs(i - 1), half)
-        for i, v in enumerate(p):
-            put(i, -(alpha[k] * v))
+        if k < n - 1:
+            for i, v in enumerate(p):
+                put(i, -(alpha[k] * v))
         if before is not None:
             for i, v in enumerate(before):
                 put(i, -(beta[k] * v))
         before, p = p, new
-    scale = one / at[n]
-    residual = [scale * v for v in p]
-    rest = [-v for v in residual]
-    rest[0] = rest[0] + one
-    q = [None] * (n + 2)
-    zero = 0.0 * one
-    q[n] = q[n + 1] = zero
-    for k in range(n, 1, -1):
-        q[k - 1] = (q[k] - rest[k]) * kappa - q[k + 1]
-    q[0] = (q[1] - rest[1]) * tau - 0.5 * q[2]
-    return q[:n], residual
+    v = before + [0.0 * one]
+    at_u = tau * at[-1] - beta[n - 1] * at[-2]
+    return p, v, without_pole(p, kappa), without_pole(v, kappa), at_u, at[-1]
 
 
 def kernel(nx, nz, sizes, r_hbm, c_hbm, a_hbm, x_out, r_out,
-           cond, absorb, diag, weight, fx, fy, fz, turned, wx, wy, wz, xadd, yadd, zadd, field, xsend, zsend, zrecv, ysend, yrecv, xrecv,
+           cond, absorb, diag, weight, fx, fy, fz, turned, wx, wy, dy, wz, xadd, yadd, zadd, field, xsend, zsend, zrecv, ysend, yrecv, xrecv,
            part1, part2, dots, table, coef,
            load_sem, face_send, face_recv, sum1_send, sum1_recv, sum2_send, sum2_recv):
     gx, gy, gz = sizes
@@ -178,11 +185,11 @@
     def turn_of(x, h):
         return 2 * x + 2 * nx * h
 
-    def pack(source):
+    def pack(source, skip=1, start=base):
         out = jnp.zeros((half, LANES), F32)
         for x in range(nx):
             for h in range(2):
-                v = source[x + 1, pl.ds(base + half * h, half), :]
+                v = source[x + skip, pl.ds(start + half * h, half), :]
                 out = jnp.where(pair == x + nx * h, pltpu.roll(v, (turn_of(x, h) + 1) % LANES, 1), out)
         return out
 
@@ -200,20 +207,24 @@
                 device_id=(ix, iy, jnp.clip(iz + 2 * up - 1, 0, gz - 1)), device_id_type=MESH))
         return xc, yc, zc
 
-    def send(e):
-        xc, yc, zc = copies(e)
+    def send_z(e):
+        _, _, zc = copies(e)
         pl.when(iz > 0)(zc[0].start)
         pl.when(iz < gz - 1)(zc[1].start)
+
+    def send_xy(e):
+        xc, yc, _ = copies(e)
         pl.when(iy > 0)(yc[0].start)
         pl.when(iy < gy - 1)(yc[1].start)
         xc.start()
 
     def send_field(source, e):
-        ysend[e] = pack(source)
         zsend[e, 0] = source[pl.ds(1, nx), base, :]
         zsend[e, 1] = source[pl.ds(1, nx), base + nz - 1, :]
+        send_z(e)
+        ysend[e] = pack(source)
         xsend[e] = source[border, inner, :]
-        send(e)
+        send_xy(e)
 
     def receive(e):
         xc, yc, zc = copies(e)
@@ -340,12 +351,10 @@
     wz[1] = weight[pl.ds(0, nx), nz - 1, :] * fz[pl.ds(0, nx), base + nz - 1, :]
 
     send_field(field.at[0], 1)
-    packed = jnp.zeros((half, LANES), F32)
-    for x in range(nx):
-        for h in range(2):
-            v = turned[x, pl.ds(half * h, half), :]
-            packed = jnp.where(pair == x + nx * h, pltpu.roll(v, (turn_of(x, h) + 1) % LANES, 1), packed)
-    wy[...] = packed
+    packed = pack(turned, 0, 0)
+    wy[0] = jnp.where(even, pltpu.roll(packed, LANES - 1, 1), 0.0)
+    wy[1] = jnp.where(even, 0.0, pltpu.roll(packed, 1, 1))
+    dy[...] = pack(diag, 0, 0)
     zadd[0] = zero_face
     zadd[1] = zero_face
     xadd[...] = zero_slab
@@ -395,20 +404,27 @@
         a_all, b_all = spread(a), spread(table[k, 1])
 
         def row(x, acc):
-            same, older = acc
+            same, older, ahead = acc
             v = field[src, x + 1, inner, :]
             y = fy[x]
             o = field[old, x + 1, inner, :]
             s = fx[x + 1] * field[src, x + 2, inner, :] + fx[x] * field[src, x, inner, :]
             s = s + fz[x, inner, :] * field[src, x + 1, above, :] + fz[x, below, :] * field[src, x + 1, below, :]
             s = s + y * pltpu.roll(v, LANES - 1, 1) + pltpu.roll(y * v, 1, 1)
-            field[dst, x + 1, inner, :] = a_all * (weight[x] * s) - b_all * o
+            new = a_all * (weight[x] * s) - b_all * o
+            field[dst, x + 1, inner, :] = new
             w = diag[x] * v
-            return same + w * v, older + w * o
-
-        same, older = lax.fori_loop(0, nx, row, (zero_slab, zero_slab), unroll=4)
+            return same + w * v, older + w * o, ahead + w * new
+
+        same, older, ahead = lax.fori_loop(0, nx, row, (zero_slab, zero_slab, zero_slab), unroll=4)
         dots[2 * k] = tile_sum(same)
         dots[2 * k + 1] = tile_sum(older)
+        dots[2 * STEPS] = tile_sum(ahead)
+
+        @pl.when(k == STEPS - 1)
+        def _():
+            sum_begin(1, one_row([dots[m if m % 2 == 0 else m + 2] for m in range(2 * STEPS - 1)]))
+
 
         ypart = pack(field.at[dst])
         zpart = [field[dst, pl.ds(1, nx), base + row_, :] for row_ in (0, nz - 1)]
@@ -416,10 +432,24 @@
 
         receive(e)
         a_half = spread(a, half)
-        sides = jnp.where(even, pltpu.roll(yrecv[e, 1], LANES - 1, 1), pltpu.roll(yrecv[e, 0], 1, 1))
-        ya = a_half * wy[...] * sides
+        low_side = a_half * wy[0] * yrecv[e, 0]
+        high_side = a_half * wy[1] * yrecv[e, 1]
         za = [a_half * wz[i] * zrecv[e, i] for i in range(2)]
         xa = a_all * wx[...] * xrecv[e]
+
+        @pl.when(k < STEPS - 1)
+        def _():
+            for h in range(2):
+                at = (half - 1) * h
+                zface = zpart[h] + za[h]
+                for at_lane, side, shift in ((0, low_side, 0), (LANES - 1, high_side, 1)):
+                    one_lane = jnp.where(face_lane == 2 * face_row + 2 * nx * h + shift, side[at:at + 1], 0.0)
+                    zface = zface + jnp.where(face_lane == at_lane, jnp.sum(one_lane, axis=1, keepdims=True), 0.0)
+                at = (nz - 1) * h
+                zsend[e + 1, h] = zface + jnp.where(face_row == border - 1, xa[at:at + 1], 0.0)
+            send_z(e + 1)
+
+        ya = jnp.where(even, pltpu.roll(high_side, LANES - 1, 1), pltpu.roll(low_side, 1, 1))
         yadd[...] = ya
         zadd[0] = za[0]
         zadd[1] = za[1]
@@ -431,7 +461,7 @@
             xlanes = []
             for h in range(2):
                 here = 2 * nx * h + 1
-                at = half_row == (nz - 1 - half) * h
+                at = half_row == (half - 1) * h
                 moved = jnp.where(face_lane // 2 == face_row + nx * h, pltpu.roll(za[h], here, 1, stride=2, stride_axis=0), 0.0)
                 yface = yface + jnp.where(at, jnp.sum(moved, axis=0, keepdims=True), 0.0)
                 xa_half = xa[half * h:half * (h + 1)]
@@ -440,45 +470,45 @@
                 yface = yface + jnp.where(pair == border - 1 + nx * h, moved, 0.0)
                 moved = jnp.where(low_x, pltpu.roll(ya, (LANES - turns[0]) % LANES, 1), pltpu.roll(ya, LANES - turns[1], 1))
                 xlanes.append(moved)
-                line_ = jnp.sum(jnp.where(at, ya, 0.0), axis=0, keepdims=True)
-                zface = zpart[h] + za[h]
-                for at_lane, shift in ((LANES - 1, 0), (0, 1)):
-                    one_lane = jnp.where(face_lane == 2 * face_row + 2 * nx * h + shift, line_, 0.0)
-                    zface = zface + jnp.where(face_lane == at_lane, jnp.sum(one_lane, axis=1, keepdims=True), 0.0)
                 z_at = slab_row == (nz - 1) * h
-                zface = zface + jnp.where(face_row == border - 1, jnp.sum(jnp.where(z_at, xa, 0.0), axis=0, keepdims=True), 0.0)
-                zsend[e + 1, h] = zface
                 xface = xface + jnp.where(z_at, jnp.sum(jnp.where(face_row == border - 1, za[h], 0.0), axis=0, keepdims=True), 0.0)
             xsend[e + 1] = xface + jnp.where(edge, jnp.concatenate(xlanes, axis=0), 0.0)
             ysend[e + 1] = yface
-            send(e + 1)
+            send_xy(e + 1)
 
         return 0
 
     lax.fori_loop(0, STEPS, step, 0)
+    last = dots[2 * STEPS] + tile_sum(xadd[...] * diag[border - 1] * xsend[STEPS])
+    faces = yadd[...] * dy[...] * ysend[STEPS]
+    for i in range(2):
+        faces = faces + zadd[i] * diag[pl.ds(0, nx), (nz - 1) * i, :] * zsend[STEPS, i]
+    sum_begin(2, one_row([last + jnp.sum(faces.reshape(half // 8, 8, LANES), axis=0)]))
     correct(STEPS)
-
-    def last_dot(x, acc):
-        return acc + diag[x] * field[STEPS, x + 1, inner, :] * field[STEPS - 1, x + 1, inner, :]
-
-    dots[2 * STEPS + 1] = tile_sum(lax.fori_loop(0, nx, last_dot, zero_slab, unroll=4))
-    sum_begin(1, one_row([dots[m if m % 2 == 0 else m + 2] for m in range(2 * STEPS)]))
     sum_middle(1)
+    sum_middle(2)
     high, low = sum_end(1)
     kappa = table[2, 0]
     half_kappa = table[2, 1]
-    raw = [(all_lanes(high, m), all_lanes(low, m)) for m in range(2 * STEPS)]
+    raw = [(all_lanes(high, m), all_lanes(low, m)) for m in range(2 * STEPS - 1)]
     exact = (half_kappa, jnp.zeros((8, LANES), F32))
     raw[1] = dmul(raw[1], exact)
     raw[2] = dmul(dmul(raw[2], exact), exact)
     raw[3] = dmul(raw[3], exact)
     mu = raw[:2]
-    for m in range(2, 2 * STEPS):
+    for m in range(2, 2 * STEPS - 1):
         mu.append(dadd(dtimes(raw[m], 2.0), dneg(mu[m % 2])))
-    alpha, beta = jacobi_matrix(mu)
-    xs, rs = solution_polynomials(alpha, beta, kappa, one)
-    xs[1] = xs[1] * half_kappa
-    rs[1] = rs[1] * half_kappa
+    alpha, beta, end, pivot, ratio = jacobi_matrix(mu)
+    u, v, xu, xv, at_u, at_v = solution_polynomials(alpha, beta, kappa, one)
+    for p in (u, v, xu, xv):
+        p[1] = p[1] * half_kappa
+    end = dadd(end, dtimes(mu[1], -(2.0 ** (2 - 2 * STEPS))))
+    high, low = sum_end(2)
+    end = dadd(end, dtimes((all_lanes(high, 0), all_lanes(low, 0)), 2.0 ** (3 - 2 * STEPS)))
+    end = dadd(ddiv(end, pivot), dneg(ratio))[0]
+    scale = one / (at_u - end * at_v)
+    xs = [scale * (p - end * q) for p, q in zip(xu, xv)]
+    rs = [scale * (p - end * q) for p, q in zip(u, v)]
     for k, v in enumerate(xs):
         coef[k] = v
     for k, v in enumerate(rs):
@@ -526,6 +556,7 @@
                 pltpu.VMEM((nx, tall, LANES), F32),
                 pltpu.VMEM(block, F32),
                 pltpu.VMEM((nz, LANES), F32),
+                pltpu.VMEM((2, nz // 2, LANES), F32),
                 pltpu.VMEM((nz // 2, LANES), F32),
                 pltpu.VMEM((2, nx, LANES), F32),
                 pltpu.VMEM((nz, LANES), F32),
@@ -538,18 +569,18 @@
                 pltpu.VMEM((exchanges, nz // 2, LANES), F32),
                 pltpu.VMEM((exchanges, 2, nz // 2, LANES), F32),
                 pltpu.VMEM((exchanges, nz, LANES), F32),
-                pltpu.VMEM((2, gx * gy, 1, LANES), F32),
-                pltpu.VMEM((2, gz, 2, LANES), F32),
+                pltpu.VMEM((3, gx * gy, 1, LANES), F32),
+                pltpu.VMEM((3, gz, 2, LANES), F32),
                 pltpu.VMEM((2 * STEPS + 2, 8, LANES), F32),
                 pltpu.VMEM((STEPS, 2, 8, LANES), F32),
                 pltpu.VMEM((32, 8, LANES), F32),
                 dma((3,)),
                 dma((exchanges, 5)),
                 dma((exchanges, 5)),
-                dma((2, gx * gy)),
-                dma((2, gx * gy)),
-                dma((2, gz)),
-                dma((2, gz)),
+                dma((3, gx * gy)),
+                dma((3, gx * gy)),
+                dma((3, gz)),
+                dma((3, gz)),
             ],
             compiler_params=pltpu.CompilerParams(
                 collective_id=0, has_side_effects=True, vmem_limit_bytes=48 * 1024 * 1024

time: 71.4 us -> 68.6 us (0.961)
  Pallas kernels: 67.8 us -> 64.9 us
    pallas_call x1, Pallas kernels: 67.8 us -> 64.9 us  [on_device(): pl.pallas_call(functools.partial(kernel, nx, nz, (gx, gy, gz)), out_shape...]
where the time goes in v4:
time: 68.6 us; the launch traced here: 67.5 us
  Pallas kernels  64.9 us (95%)
  local copies, waits for them, and re-layouts  1.94 us (3%)
    pallas_call x1, Pallas kernels, on_device(): pl.pallas_call(functools.partial(kernel, nx, nz, (gx, gy, gz)), out_shape...  64.9 us
    unnamed x2, local copies, waits for them, and re-layouts  1.94 us

profile of v4, /device:TPU:8, one launch (start us, length us, event | category | flops | bytes accessed | tf_op | source)
XLA Modules:
  0.0 67.5 jit_solution(17310551018068349636)
XLA Ops:
  0.6 64.9 %shard_map.50 = (f32[32,64,128]{2,1,0:T(8,128)S(1)}, f32[32,64,128]{2,1,0:T(8,128)S(1)}) custom-call(f32[32,64,128]{2,1,0:T(8,128)} %bitcast.7, f32[32,64,128]{2,1,0:T(8,128)} %bitcast.8, f32[32,64,128]{2,1,0:T(8,128)} %bitcast.9), custom_call_target="tpu_custom_call" | custom-call | tf_op jit(solution)/shard_map/pallas_call | solution.py:544
  65.6 1.0 %copy.7 = f32[32,128,64]{1,2,0:T(8,128)} copy(f32[32,128,64]{1,2,0:T(8,128)S(1)} %bitcast.6) | data formatting | bytes 2097152
  66.5 1.0 %copy.8 = f32[32,128,64]{1,2,0:T(8,128)} copy(f32[32,128,64]{1,2,0:T(8,128)S(1)} %bitcast.5) | data formatting | bytes 2097152

commit v5 on v4

--- a/solution.py
+++ b/solution.py
@@ -128,9 +128,9 @@
     return p, v, without_pole(p, kappa), without_pole(v, kappa), at_u, at[-1]
 
 
-def kernel(nx, nz, sizes, r_hbm, c_hbm, a_hbm, x_out, r_out,
-           cond, absorb, diag, weight, fx, fy, fz, turned, wx, wy, dy, wz, xadd, yadd, zadd, field, xsend, zsend, zrecv, ysend, yrecv, xrecv,
-           part1, part2, dots, table, coef,
+def kernel(nx, nz, sizes, r_hbm, c_hbm, a_hbm, field, diag, coef,
+           cond, absorb, weight, fx, fy, fz, turned, wx, wy, dy, wz, xadd, yadd, zadd, xsend, zsend, zrecv, ysend, yrecv, xrecv,
+           part1, part2, dots, table,
            load_sem, face_send, face_recv, sum1_send, sum1_recv, sum2_send, sum2_recv):
     gx, gy, gz = sizes
     ix, iy, iz = lax.axis_index("gx"), lax.axis_index("gy"), lax.axis_index("gz")
@@ -147,7 +147,7 @@
     loads = [
         pltpu.make_async_copy(c_hbm, cond.at[pl.ds(1, nx), inner, :], load_sem.at[0]),
         pltpu.make_async_copy(a_hbm, absorb, load_sem.at[1]),
-        pltpu.make_async_copy(r_hbm, r_out, load_sem.at[2]),
+        pltpu.make_async_copy(r_hbm, weight, load_sem.at[2]),
     ]
     for load in loads:
         load.start()
@@ -218,13 +218,13 @@
         pl.when(iy < gy - 1)(yc[1].start)
         xc.start()
 
-    def send_field(source, e):
+    def fill_z(source, e):
         zsend[e, 0] = source[pl.ds(1, nx), base, :]
         zsend[e, 1] = source[pl.ds(1, nx), base + nz - 1, :]
-        send_z(e)
+
+    def fill_xy(source, e):
         ysend[e] = pack(source)
         xsend[e] = source[border, inner, :]
-        send_xy(e)
 
     def receive(e):
         xc, yc, zc = copies(e)
@@ -248,14 +248,19 @@
                 part.at[which, mine], part.at[which, mine], send_sem.at[which, i], recv_sem.at[which, mine],
                 device_id=peer, device_id_type=MESH).start()
 
-    def gather_in(stage, which):
+    def arrivals(stage, which):
         part, peers, _, send_sem, recv_sem, slots = stage
-        for i, slot in enumerate(slots):
-            copy = pltpu.make_async_remote_copy(
+        return [
+            pltpu.make_async_remote_copy(
                 part.at[which, slot], part.at[which, slot], send_sem.at[which, i], recv_sem.at[which, slot],
                 device_id=peers[i], device_id_type=MESH)
+            for i, slot in enumerate(slots)
+        ]
+
+    def gather_in(stage, which):
+        part = stage[0]
+        for copy in arrivals(stage, which):
             copy.wait_recv()
-            copy.wait_send()
         total, error = part[which, 0], jnp.zeros_like(part[which, 0])
         for i in range(1, part.shape[1]):
             total, e = two_sum(total, part[which, i])
@@ -287,12 +292,16 @@
 
     wide_lane = lax.broadcasted_iota(jnp.int32, (nz, LANES), 1)
     inside = wide_lane < LANES - 1
+    after = wide_lane > 0
     edge = (wide_lane == 0) | (wide_lane == LANES - 1)
     one = jnp.ones((8, LANES), F32)
 
     loads[0].wait()
     pl.semaphore_wait(barrier, len(group) + len(line))
-    send_field(cond, 0)
+    fill_z(cond, 0)
+    send_z(0)
+    fill_xy(cond, 0)
+    send_xy(0)
     loads[1].wait()
 
     def means(x, acc):
@@ -330,10 +339,11 @@
         xp = 0.5 * (here + cond[x + 2, inner, :])
         xm = fx[x]
         yp = jnp.where(inside, 0.5 * (here + pltpu.roll(here, LANES - 1, 1)), 0.0)
+        ym = jnp.where(after, 0.5 * (here + pltpu.roll(here, 1, 1)), 0.0)
         ye = jnp.where(edge, 0.5 * (here + turned[x]), 0.0)
         zp = 0.5 * (here + cond[x + 1, above, :])
         zm = 0.5 * (here + cond[x + 1, below, :])
-        total = absorb[x] + xp + xm + yp + pltpu.roll(yp, 1, 1) + ye + zp + zm
+        total = absorb[x] + xp + xm + yp + ym + ye + zp + zm
         inverse = 1.0 / total
         fx[x + 1] = xp
         fy[x] = yp
@@ -341,16 +351,19 @@
         fz[x, below, :] = zm
         fz[x, inner, :] = zp
         diag[x] = total
+        field[0, x + 1, inner, :] = weight[x] * inverse
         weight[x] = inverse
-        field[0, x + 1, inner, :] = r_out[x] * inverse
         return 0
 
-    lax.fori_loop(0, nx, coefficients, 0, unroll=2)
+    lax.fori_loop(0, nx, coefficients, 0, unroll=8)
     wx[...] = weight[border - 1] * fx[jnp.where(low_x, nx, 0)]
     wz[0] = weight[pl.ds(0, nx), 0, :] * fz[pl.ds(0, nx), base - 1, :]
     wz[1] = weight[pl.ds(0, nx), nz - 1, :] * fz[pl.ds(0, nx), base + nz - 1, :]
 
-    send_field(field.at[0], 1)
+    fill_z(field.at[0], 1)
+    send_z(1)
+    fill_xy(field.at[0], 1)
+    send_xy(1)
     packed = pack(turned, 0, 0)
     wy[0] = jnp.where(even, pltpu.roll(packed, LANES - 1, 1), 0.0)
     wy[1] = jnp.where(even, 0.0, pltpu.roll(packed, 1, 1))
@@ -513,8 +526,20 @@
         coef[k] = v
     for k, v in enumerate(rs):
         coef[16 + k] = v
-
-    def finish(x, _):
+    for which in range(3):
+        for stage in (first, second):
+            for copy in arrivals(stage, which):
+                copy.wait_send()
+
+
+def finish(nx, nz, groups, field, diag, coef, x_hbm, r_hbm, xs, rs, sems):
+    inner = pl.ds(BASE, nz)
+    size = nx // groups
+
+    def spread(c):
+        return jnp.broadcast_to(c[None], (nz // 8, 8, LANES)).reshape(nz, LANES)
+
+    def slab(x, _):
         v = field[0, x + 1, inner, :]
         sx = spread(coef[0]) * v
         sr = spread(coef[16]) * v
@@ -523,11 +548,20 @@
             if k < STEPS:
                 sx = sx + spread(coef[k]) * v
             sr = sr + spread(coef[16 + k]) * v
-        x_out[x] = sx
-        r_out[x] = diag[x] * sr
+        xs[x] = sx
+        rs[x] = diag[x] * sr
         return 0
 
-    lax.fori_loop(0, nx, finish, 0)
+    copies = []
+    for g in range(groups):
+        lax.fori_loop(g * size, (g + 1) * size, slab, 0, unroll=2)
+        part = pl.ds(g * size, size)
+        for n, (src, dst) in enumerate(((xs, x_hbm), (rs, r_hbm))):
+            copy = pltpu.make_async_copy(src.at[part], dst.at[part], sems.at[n, g])
+            copy.start()
+            copies.append(copy)
+    for copy in copies:
+        copy.wait()
 
 
 def solution(mesh):
@@ -541,14 +575,15 @@
         exchanges = STEPS + 1
         dma = pltpu.SemaphoreType.DMA
         tall = nz + 16
-        out = pl.pallas_call(
+        field = (STEPS + 1, nx + 2, tall, LANES)
+        vmem = pl.BlockSpec(memory_space=pltpu.VMEM)
+        kept = pl.pallas_call(
             functools.partial(kernel, nx, nz, (gx, gy, gz)),
-            out_shape=[jax.ShapeDtypeStruct(block, F32)] * 2,
+            out_shape=[pltpu.VMEM(field, F32), pltpu.VMEM(block, F32), pltpu.VMEM((32, 8, LANES), F32)],
             in_specs=[pl.BlockSpec(memory_space=pl.ANY)] * 3,
-            out_specs=[pl.BlockSpec(memory_space=pltpu.VMEM)] * 2,
+            out_specs=[vmem] * 3,
             scratch_shapes=[
                 pltpu.VMEM((nx + 2, tall, LANES), F32),
-                pltpu.VMEM(block, F32),
                 pltpu.VMEM(block, F32),
                 pltpu.VMEM(block, F32),
                 pltpu.VMEM((nx + 1, nz, LANES), F32),
@@ -562,7 +597,6 @@
                 pltpu.VMEM((nz, LANES), F32),
                 pltpu.VMEM((nz // 2, LANES), F32),
                 pltpu.VMEM((2, nx, LANES), F32),
-                pltpu.VMEM((STEPS + 1, nx + 2, tall, LANES), F32),
                 pltpu.VMEM((exchanges, nz, LANES), F32),
                 pltpu.VMEM((exchanges, 2, nx, LANES), F32),
                 pltpu.VMEM((exchanges, 2, nx, LANES), F32),
@@ -573,7 +607,6 @@
                 pltpu.VMEM((3, gz, 2, LANES), F32),
                 pltpu.VMEM((2 * STEPS + 2, 8, LANES), F32),
                 pltpu.VMEM((STEPS, 2, 8, LANES), F32),
-                pltpu.VMEM((32, 8, LANES), F32),
                 dma((3,)),
                 dma((exchanges, 5)),
                 dma((exchanges, 5)),
@@ -583,9 +616,18 @@
                 dma((3, gz)),
             ],
             compiler_params=pltpu.CompilerParams(
-                collective_id=0, has_side_effects=True, vmem_limit_bytes=48 * 1024 * 1024
+                collective_id=0, has_side_effects=True, vmem_limit_bytes=40 * 1024 * 1024
             ),
         )(*[pltpu.with_memory_space_constraint(v, pltpu.HBM) for v in args])
+        groups = 4
+        out = pl.pallas_call(
+            functools.partial(finish, nx, nz, groups),
+            out_shape=[jax.ShapeDtypeStruct(block, F32)] * 2,
+            in_specs=[vmem] * 3,
+            out_specs=[pl.BlockSpec(memory_space=pltpu.HBM)] * 2,
+            scratch_shapes=[pltpu.VMEM(block, F32), pltpu.VMEM(block, F32), dma((2, groups))],
+            compiler_params=pltpu.CompilerParams(vmem_limit_bytes=20 * 1024 * 1024),
+        )(*kept)
         return tuple(jnp.transpose(v, (0, 2, 1)) for v in out)
 
     spec = P("gx", "gy", "gz")

time: 68.6 us -> 65.7 us (0.958)
  local copies, waits for them, and re-layouts: 1.94 us -> 0 us
  Pallas kernels: 64.9 us -> 64 us
    pallas_call x1, Pallas kernels: 64.9 us -> 61.6 us  [on_device(): pl.pallas_call(functools.partial(kernel, nx, nz, (gx, gy, gz)), out_shape...]
    pallas_call x0 -> x1, Pallas kernels: none -> 2.47 us  [on_device(): pl.pallas_call(functools.partial(finish, nx, nz, groups), out_shape=[jax....]
    unnamed x2 -> x0, local copies, waits for them, and re-layouts: 1.94 us -> none
where the time goes in v5:
time: 65.7 us; the launch traced here: 64.7 us
  Pallas kernels  64 us (97%)
    pallas_call x1, Pallas kernels, on_device(): pl.pallas_call(functools.partial(kernel, nx, nz, (gx, gy, gz)), out_shape...  61.6 us
    pallas_call x1, Pallas kernels, on_device(): pl.pallas_call(functools.partial(finish, nx, nz, groups), out_shape=[jax....  2.47 us

profile of v5, /device:TPU:8, one launch (start us, length us, event | category | flops | bytes accessed | tf_op | source)
XLA Modules:
  0.0 64.7 jit_solution(7906021940618201139)
XLA Ops:
  0.6 61.6 %shard_map.50 = (f32[11,34,80,128]{3,2,1,0:T(8,128)S(1)}, f32[32,64,128]{2,1,0:T(8,128)S(1)}, f32[32,8,128]{2,1,0:T(8,128)S(1)}) custom-call(f32[32,64,128]{2,1,0:T(8,128)} %bitcast.5, f32[32,64,128]{2,1,0:T(8,128)} %bitcast.6, f32[32,64,128]{2,1,0:T(8,128)} %bitcast.7), custom_call_target="tpu_custom_call" | custom-call | tf_op jit(solution)/shard_map/pallas_call | solution.py:580
  62.2 2.5 %shard_map.51 = (f32[32,64,128]{2,1,0:T(8,128)}, f32[32,64,128]{2,1,0:T(8,128)}) custom-call(f32[11,34,80,128]{3,2,1,0:T(8,128)S(1)} %get-tuple-element.7.field, f32[32,64,128]{2,1,0:T(8,128)S(1)} %get-tuple-element.8.diag, f32[32,8,128]{2,1,0:T(8,128)S(1)} %get-tuple-element.9.coef), custom_call_target="tpu_custom_call" | custom-call | tf_op jit(solution)/shard_map/pallas_call | solution.py:623

commit v6 on v5

--- a/solution.py
+++ b/solution.py
@@ -234,9 +234,6 @@
         pl.when(iz > 0)(lambda: (zc[0].wait_send(), zc[1].wait_recv())[0])
         pl.when(iz < gz - 1)(lambda: (zc[1].wait_send(), zc[0].wait_recv())[0])
 
-    def beside(e):
-        return jnp.where(even, yrecv[e, 0], pltpu.roll(yrecv[e, 1], LANES - 2, 1))
-
     gxy = ix * gy + iy
     first = (part1, [(px, py, iz) for px, py in group], gxy, sum1_send, sum1_recv, [px * gy + py for px, py in group])
     second = (part2, [(ix, iy, pz) for pz in line], iz, sum2_send, sum2_recv, line)
@@ -296,6 +293,65 @@
     edge = (wide_lane == 0) | (wide_lane == LANES - 1)
     one = jnp.ones((8, LANES), F32)
 
+    face_row = lax.broadcasted_iota(jnp.int32, (nx, LANES), 0)
+    face_lane = lax.broadcasted_iota(jnp.int32, (nx, LANES), 1)
+    half_row = lax.broadcasted_iota(jnp.int32, (half, LANES), 0)
+    slab_row = lax.broadcasted_iota(jnp.int32, (nz, LANES), 0)
+
+    def z_faces(zpart, za, low_side, high_side, xa):
+        faces = []
+        for h in range(2):
+            at = (half - 1) * h
+            face = zpart[h] + za[h]
+            for at_lane, side, shift in ((0, low_side, 0), (LANES - 1, high_side, 1)):
+                one_lane = jnp.where(face_lane == 2 * face_row + 2 * nx * h + shift, side[at:at + 1], 0.0)
+                face = face + jnp.where(face_lane == at_lane, jnp.sum(one_lane, axis=1, keepdims=True), 0.0)
+            at = (nz - 1) * h
+            faces.append(face + jnp.where(face_row == border - 1, xa[at:at + 1], 0.0))
+        return faces
+
+    def joined(low_side, high_side):
+        return jnp.where(even, pltpu.roll(high_side, LANES - 1, 1), pltpu.roll(low_side, 1, 1))
+
+    def xy_faces(xpart, ypart, za, ya, xa):
+        yface, xface = ypart + ya, xpart + xa
+        xlanes = []
+        for h in range(2):
+            here = 2 * nx * h + 1
+            at = half_row == (half - 1) * h
+            moved = jnp.where(face_lane // 2 == face_row + nx * h, pltpu.roll(za[h], here, 1, stride=2, stride_axis=0), 0.0)
+            yface = yface + jnp.where(at, jnp.sum(moved, axis=0, keepdims=True), 0.0)
+            xa_half = xa[half * h:half * (h + 1)]
+            turns = [(2 * (nx - 1) + here) % LANES, here]
+            moved = jnp.where(low_x, pltpu.roll(xa_half, turns[0], 1), pltpu.roll(xa_half, turns[1], 1))
+            yface = yface + jnp.where(pair == border - 1 + nx * h, moved, 0.0)
+            moved = jnp.where(low_x, pltpu.roll(ya, (LANES - turns[0]) % LANES, 1), pltpu.roll(ya, LANES - turns[1], 1))
+            xlanes.append(moved)
+            z_at = slab_row == (nz - 1) * h
+            xface = xface + jnp.where(z_at, jnp.sum(jnp.where(face_row == border - 1, za[h], 0.0), axis=0, keepdims=True), 0.0)
+        return xface + jnp.where(edge, jnp.concatenate(xlanes, axis=0), 0.0), yface
+
+    def keep(za, ya, xa):
+        yadd[...] = ya
+        zadd[0] = za[0]
+        zadd[1] = za[1]
+        xadd[...] = xa
+
+    def correct(ref, skip=1, start=base):
+        ref[pl.ds(skip, nx), start, :] += zadd[0]
+        ref[pl.ds(skip, nx), start + nz - 1, :] += zadd[1]
+        ref[border - 1 + skip, pl.ds(start, nz), :] += xadd[...]
+        terms = yadd[...]
+        for x in range(nx):
+            for h in range(2):
+                turned[x, pl.ds(half * h, half), :] = pltpu.roll(terms, (LANES - turn_of(x, h) - 1) % LANES, 1)
+
+        def add_sides(x, _):
+            ref[x + skip, pl.ds(start, nz), :] += jnp.where(edge, turned[x], 0.0)
+            return 0
+
+        lax.fori_loop(0, nx, add_sides, 0, unroll=4)
+
     loads[0].wait()
     pl.semaphore_wait(barrier, len(group) + len(line))
     fill_z(cond, 0)
@@ -320,78 +376,62 @@
     lax.fori_loop(0, STEPS, clear, 0)
     table[0, 0] = one
     table[0, 1] = jnp.zeros((8, LANES), F32)
-    loads[2].wait()
-    receive(0)
-    sum_middle(0)
-
-    cond[jnp.where(low_x, nx + 1, 0), inner, :] = xrecv[0]
-    cond[jnp.where(low_x, 0, nx + 1), inner, :] = zero_slab
-    cond[pl.ds(1, nx), base - 1, :] = zrecv[0, 0]
-    cond[pl.ds(1, nx), base + nz, :] = zrecv[0, 1]
-    for_c = beside(0)
-    for x in range(nx):
-        for h in range(2):
-            turned[x, pl.ds(half * h, half), :] = pltpu.roll(for_c, (LANES - turn_of(x, h)) % LANES, 1)
-    fx[0] = 0.5 * (cond[0, inner, :] + cond[1, inner, :])
+    cond[0, inner, :] = zero_slab
+    cond[nx + 1, inner, :] = zero_slab
+    cond[pl.ds(1, nx), base - 1, :] = zero_face
+    cond[pl.ds(1, nx), base + nz, :] = zero_face
+    fx[0] = 0.5 * cond[1, inner, :]
 
     def coefficients(x, _):
         here = cond[x + 1, inner, :]
         xp = 0.5 * (here + cond[x + 2, inner, :])
         xm = fx[x]
-        yp = jnp.where(inside, 0.5 * (here + pltpu.roll(here, LANES - 1, 1)), 0.0)
-        ym = jnp.where(after, 0.5 * (here + pltpu.roll(here, 1, 1)), 0.0)
-        ye = jnp.where(edge, 0.5 * (here + turned[x]), 0.0)
+        yp = 0.5 * (here + jnp.where(inside, pltpu.roll(here, LANES - 1, 1), 0.0))
+        ym = 0.5 * (here + jnp.where(after, pltpu.roll(here, 1, 1), 0.0))
         zp = 0.5 * (here + cond[x + 1, above, :])
         zm = 0.5 * (here + cond[x + 1, below, :])
-        total = absorb[x] + xp + xm + yp + ym + ye + zp + zm
-        inverse = 1.0 / total
         fx[x + 1] = xp
-        fy[x] = yp
-        turned[x] = ye * inverse
+        fy[x] = jnp.where(inside, yp, 0.0)
         fz[x, below, :] = zm
         fz[x, inner, :] = zp
-        diag[x] = total
+        diag[x] = absorb[x] + xp + xm + yp + ym + zp + zm
+        return 0
+
+    lax.fori_loop(0, nx, coefficients, 0, unroll=8)
+    loads[2].wait()
+    ypart, yright = pack(diag, 0, 0), pack(weight, 0, 0)
+    receive(0)
+    low_side, high_side = 0.5 * yrecv[0, 0], 0.5 * yrecv[0, 1]
+    za = [0.5 * zrecv[0, i] for i in range(2)]
+    xa = 0.5 * xrecv[0]
+    zdiag = z_faces([diag[pl.ds(0, nx), (nz - 1) * i, :] for i in range(2)], za, low_side, high_side, xa)
+    for i in range(2):
+        zsend[1, i] = weight[pl.ds(0, nx), (nz - 1) * i, :] / zdiag[i]
+    send_z(1)
+    ya = joined(low_side, high_side)
+    xdiag, ydiag = xy_faces(diag[border - 1], ypart, za, ya, xa)
+    xsend[1] = weight[border - 1] / xdiag
+    ysend[1] = yright / ydiag
+    send_xy(1)
+    sum_middle(0)
+    for i in range(2):
+        wz[i] = (0.5 * zsend[0, i] + za[i]) / zdiag[i]
+    wx[...] = (0.5 * xsend[0] + xa) / xdiag
+    sides = (0.5 * ysend[0] + ya) / ydiag
+    wy[0] = jnp.where(even, pltpu.roll(sides, LANES - 1, 1), 0.0)
+    wy[1] = jnp.where(even, 0.0, pltpu.roll(sides, 1, 1))
+    dy[...] = ydiag
+    keep(za, ya, xa)
+    correct(diag, 0, 0)
+
+    def begin(x, _):
+        inverse = 1.0 / diag[x]
         field[0, x + 1, inner, :] = weight[x] * inverse
         weight[x] = inverse
         return 0
 
-    lax.fori_loop(0, nx, coefficients, 0, unroll=8)
-    wx[...] = weight[border - 1] * fx[jnp.where(low_x, nx, 0)]
-    wz[0] = weight[pl.ds(0, nx), 0, :] * fz[pl.ds(0, nx), base - 1, :]
-    wz[1] = weight[pl.ds(0, nx), nz - 1, :] * fz[pl.ds(0, nx), base + nz - 1, :]
-
-    fill_z(field.at[0], 1)
-    send_z(1)
-    fill_xy(field.at[0], 1)
-    send_xy(1)
-    packed = pack(turned, 0, 0)
-    wy[0] = jnp.where(even, pltpu.roll(packed, LANES - 1, 1), 0.0)
-    wy[1] = jnp.where(even, 0.0, pltpu.roll(packed, 1, 1))
-    dy[...] = pack(diag, 0, 0)
-    zadd[0] = zero_face
-    zadd[1] = zero_face
-    xadd[...] = zero_slab
-    yadd[...] = jnp.zeros((half, LANES), F32)
-
-    face_row = lax.broadcasted_iota(jnp.int32, (nx, LANES), 0)
-    face_lane = lax.broadcasted_iota(jnp.int32, (nx, LANES), 1)
-    half_row = lax.broadcasted_iota(jnp.int32, (half, LANES), 0)
-    slab_row = lax.broadcasted_iota(jnp.int32, (nz, LANES), 0)
-
-    def correct(k):
-        field[k, pl.ds(1, nx), base, :] += zadd[0]
-        field[k, pl.ds(1, nx), base + nz - 1, :] += zadd[1]
-        field[k, border, inner, :] += xadd[...]
-        terms = yadd[...]
-        for x in range(nx):
-            for h in range(2):
-                turned[x, pl.ds(half * h, half), :] = pltpu.roll(terms, (LANES - turn_of(x, h) - 1) % LANES, 1)
-
-        def add_sides(x, _):
-            field[k, x + 1, inner, :] += jnp.where(edge, turned[x], 0.0)
-            return 0
-
-        lax.fori_loop(0, nx, add_sides, 0, unroll=4)
+    lax.fori_loop(0, nx, begin, 0, unroll=4)
+    keep([zero_face, zero_face], jnp.zeros((half, LANES), F32), zero_slab)
 
     def step(k, _):
         src, dst, old = k, k + 1, jnp.maximum(k - 1, 0)
@@ -412,7 +452,7 @@
                 table[j, 0] = kappa
                 table[j, 1] = one
 
-        correct(k)
+        correct(field.at[k])
         a = table[k, 0]
         a_all, b_all = spread(a), spread(table[k, 1])
 
@@ -452,41 +492,16 @@
 
         @pl.when(k < STEPS - 1)
         def _():
-            for h in range(2):
-                at = (half - 1) * h
-                zface = zpart[h] + za[h]
-                for at_lane, side, shift in ((0, low_side, 0), (LANES - 1, high_side, 1)):
-                    one_lane = jnp.where(face_lane == 2 * face_row + 2 * nx * h + shift, side[at:at + 1], 0.0)
-                    zface = zface + jnp.where(face_lane == at_lane, jnp.sum(one_lane, axis=1, keepdims=True), 0.0)
-                at = (nz - 1) * h
-                zsend[e + 1, h] = zface + jnp.where(face_row == border - 1, xa[at:at + 1], 0.0)
+            for i, face in enumerate(z_faces(zpart, za, low_side, high_side, xa)):
+                zsend[e + 1, i] = face
             send_z(e + 1)
 
-        ya = jnp.where(even, pltpu.roll(high_side, LANES - 1, 1), pltpu.roll(low_side, 1, 1))
-        yadd[...] = ya
-        zadd[0] = za[0]
-        zadd[1] = za[1]
-        xadd[...] = xa
+        ya = joined(low_side, high_side)
+        keep(za, ya, xa)
 
         @pl.when(k < STEPS - 1)
         def _():
-            yface, xface = ypart + ya, xpart + xa
-            xlanes = []
-            for h in range(2):
-                here = 2 * nx * h + 1
-                at = half_row == (half - 1) * h
-                moved = jnp.where(face_lane // 2 == face_row + nx * h, pltpu.roll(za[h], here, 1, stride=2, stride_axis=0), 0.0)
-                yface = yface + jnp.where(at, jnp.sum(moved, axis=0, keepdims=True), 0.0)
-                xa_half = xa[half * h:half * (h + 1)]
-                turns = [(2 * (nx - 1) + here) % LANES, here]
-                moved = jnp.where(low_x, pltpu.roll(xa_half, turns[0], 1), pltpu.roll(xa_half, turns[1], 1))
-                yface = yface + jnp.where(pair == border - 1 + nx * h, moved, 0.0)
-                moved = jnp.where(low_x, pltpu.roll(ya, (LANES - turns[0]) % LANES, 1), pltpu.roll(ya, LANES - turns[1], 1))
-                xlanes.append(moved)
-                z_at = slab_row == (nz - 1) * h
-                xface = xface + jnp.where(z_at, jnp.sum(jnp.where(face_row == border - 1, za[h], 0.0), axis=0, keepdims=True), 0.0)
-            xsend[e + 1] = xface + jnp.where(edge, jnp.concatenate(xlanes, axis=0), 0.0)
-            ysend[e + 1] = yface
+            xsend[e + 1], ysend[e + 1] = xy_faces(xpart, ypart, za, ya, xa)
             send_xy(e + 1)
 
         return 0
@@ -497,7 +512,7 @@
     for i in range(2):
         faces = faces + zadd[i] * diag[pl.ds(0, nx), (nz - 1) * i, :] * zsend[STEPS, i]
     sum_begin(2, one_row([last + jnp.sum(faces.reshape(half // 8, 8, LANES), axis=0)]))
-    correct(STEPS)
+    correct(field.at[STEPS])
     sum_middle(1)
     sum_middle(2)
     high, low = sum_end(1)

time: 65.7 us -> 64.2 us (0.977)
  Pallas kernels: 64 us -> 62.5 us
    pallas_call x1, Pallas kernels: 61.6 us -> 60 us  [on_device(): pl.pallas_call(functools.partial(kernel, nx, nz, (gx, gy, gz)), out_shape...]
where the time goes in v6:
time: 64.2 us; the launch traced here: 63.2 us
  Pallas kernels  62.5 us (97%)
    pallas_call x1, Pallas kernels, on_device(): pl.pallas_call(functools.partial(kernel, nx, nz, (gx, gy, gz)), out_shape...  60 us
    pallas_call x1, Pallas kernels, on_device(): pl.pallas_call(functools.partial(finish, nx, nz, groups), out_shape=[jax....  2.47 us

profile of v6, /device:TPU:8, one launch (start us, length us, event | category | flops | bytes accessed | tf_op | source)
XLA Modules:
  0.0 63.2 jit_solution(13953786421919102615)
XLA Ops:
  0.6 60.0 %shard_map.50 = (f32[11,34,80,128]{3,2,1,0:T(8,128)S(1)}, f32[32,64,128]{2,1,0:T(8,128)S(1)}, f32[32,8,128]{2,1,0:T(8,128)S(1)}) custom-call(f32[32,64,128]{2,1,0:T(8,128)} %bitcast.5, f32[32,64,128]{2,1,0:T(8,128)} %bitcast.6, f32[32,64,128]{2,1,0:T(8,128)} %bitcast.7), custom_call_target="tpu_custom_call" | custom-call | tf_op jit(solution)/shard_map/pallas_call | solution.py:595
  60.7 2.5 %shard_map.51 = (f32[32,64,128]{2,1,0:T(8,128)}, f32[32,64,128]{2,1,0:T(8,128)}) custom-call(f32[11,34,80,128]{3,2,1,0:T(8,128)S(1)} %get-tuple-element.7.field, f32[32,64,128]{2,1,0:T(8,128)S(1)} %get-tuple-element.8.diag, f32[32,8,128]{2,1,0:T(8,128)S(1)} %get-tuple-element.9.coef), custom_call_target="tpu_custom_call" | custom-call | tf_op jit(solution)/shard_map/pallas_call | solution.py:638

commit v7 on v6

--- a/solution.py
+++ b/solution.py
@@ -149,19 +149,10 @@
         pltpu.make_async_copy(a_hbm, absorb, load_sem.at[1]),
         pltpu.make_async_copy(r_hbm, weight, load_sem.at[2]),
     ]
-    for load in loads:
-        load.start()
+    loads[0].start()
 
     zero_face = jnp.zeros((nx, LANES), F32)
     zero_slab = jnp.zeros((nz, LANES), F32)
-
-    def clear_faces(k, _):
-        for side in range(2):
-            zrecv[k, side] = zero_face
-            yrecv[k, side] = zero_face
-        return 0
-
-    lax.fori_loop(0, STEPS + 1, clear_faces, 0)
 
     barrier = pltpu.get_barrier_semaphore()
     group = [((ix + dx) % gx, (iy + dy) % gy) for dx in range(gx) for dy in range(gy) if (dx, dy) != (0, 0)]
@@ -170,6 +161,16 @@
         pl.semaphore_signal(barrier, inc=1, device_id=(px, py, iz), device_id_type=MESH)
     for pz in line:
         pl.semaphore_signal(barrier, inc=1, device_id=(ix, iy, pz), device_id_type=MESH)
+
+    for ref, side, alone in ((zrecv, 0, iz == 0), (zrecv, 1, iz == gz - 1), (yrecv, 0, iy == 0), (yrecv, 1, iy == gy - 1)):
+
+        @pl.when(alone)
+        def _(ref=ref, side=side):
+            def clear_faces(k, _):
+                ref[k, side] = zero_face
+                return 0
+
+            lax.fori_loop(0, STEPS + 1, clear_faces, 0)
 
     lane = lax.broadcasted_iota(jnp.int32, (half, LANES), 1)
     pair = lane // 2
@@ -226,11 +227,14 @@
         ysend[e] = pack(source)
         xsend[e] = source[border, inner, :]
 
-    def receive(e):
-        xc, yc, zc = copies(e)
+    def receive_xy(e):
+        xc, yc, _ = copies(e)
         xc.wait()
         pl.when(iy > 0)(lambda: (yc[0].wait_send(), yc[1].wait_recv())[0])
         pl.when(iy < gy - 1)(lambda: (yc[1].wait_send(), yc[0].wait_recv())[0])
+
+    def receive_z(e):
+        _, _, zc = copies(e)
         pl.when(iz > 0)(lambda: (zc[0].wait_send(), zc[1].wait_recv())[0])
         pl.when(iz < gz - 1)(lambda: (zc[1].wait_send(), zc[0].wait_recv())[0])
 
@@ -298,11 +302,11 @@
     half_row = lax.broadcasted_iota(jnp.int32, (half, LANES), 0)
     slab_row = lax.broadcasted_iota(jnp.int32, (nz, LANES), 0)
 
-    def z_faces(zpart, za, low_side, high_side, xa):
+    def z_edges(zpart, low_side, high_side, xa):
         faces = []
         for h in range(2):
             at = (half - 1) * h
-            face = zpart[h] + za[h]
+            face = zpart[h]
             for at_lane, side, shift in ((0, low_side, 0), (LANES - 1, high_side, 1)):
                 one_lane = jnp.where(face_lane == 2 * face_row + 2 * nx * h + shift, side[at:at + 1], 0.0)
                 face = face + jnp.where(face_lane == at_lane, jnp.sum(one_lane, axis=1, keepdims=True), 0.0)
@@ -353,6 +357,8 @@
         lax.fori_loop(0, nx, add_sides, 0, unroll=4)
 
     loads[0].wait()
+    loads[1].start()
+    loads[2].start()
     pl.semaphore_wait(barrier, len(group) + len(line))
     fill_z(cond, 0)
     send_z(0)
@@ -400,13 +406,17 @@
     lax.fori_loop(0, nx, coefficients, 0, unroll=8)
     loads[2].wait()
     ypart, yright = pack(diag, 0, 0), pack(weight, 0, 0)
-    receive(0)
+    zpart = [diag[pl.ds(0, nx), (nz - 1) * i, :] for i in range(2)]
+    zright = [weight[pl.ds(0, nx), (nz - 1) * i, :] for i in range(2)]
+    receive_xy(0)
     low_side, high_side = 0.5 * yrecv[0, 0], 0.5 * yrecv[0, 1]
+    xa = 0.5 * xrecv[0]
+    zpart = z_edges(zpart, low_side, high_side, xa)
+    receive_z(0)
     za = [0.5 * zrecv[0, i] for i in range(2)]
-    xa = 0.5 * xrecv[0]
-    zdiag = z_faces([diag[pl.ds(0, nx), (nz - 1) * i, :] for i in range(2)], za, low_side, high_side, xa)
+    zdiag = [zpart[i] + za[i] for i in range(2)]
     for i in range(2):
-        zsend[1, i] = weight[pl.ds(0, nx), (nz - 1) * i, :] / zdiag[i]
+        zsend[1, i] = zright[i] / zdiag[i]
     send_z(1)
     ya = joined(low_side, high_side)
     xdiag, ydiag = xy_faces(diag[border - 1], ypart, za, ya, xa)
@@ -483,17 +493,20 @@
         zpart = [field[dst, pl.ds(1, nx), base + row_, :] for row_ in (0, nz - 1)]
         xpart = field[dst, border, inner, :]
 
-        receive(e)
         a_half = spread(a, half)
+        receive_xy(e)
         low_side = a_half * wy[0] * yrecv[e, 0]
         high_side = a_half * wy[1] * yrecv[e, 1]
-        za = [a_half * wz[i] * zrecv[e, i] for i in range(2)]
         xa = a_all * wx[...] * xrecv[e]
+        zpart = z_edges(zpart, low_side, high_side, xa)
+        zscale = [a_half * wz[i] for i in range(2)]
+        receive_z(e)
+        za = [zscale[i] * zrecv[e, i] for i in range(2)]
 
         @pl.when(k < STEPS - 1)
         def _():
-            for i, face in enumerate(z_faces(zpart, za, low_side, high_side, xa)):
-                zsend[e + 1, i] = face
+            for i in range(2):
+                zsend[e + 1, i] = zpart[i] + za[i]
             send_z(e + 1)
 
         ya = joined(low_side, high_side)

time: 64.2 us -> 63.2 us (0.984)
  Pallas kernels: 62.5 us -> 61.5 us
    pallas_call x1, Pallas kernels: 60 us -> 59 us  [on_device(): pl.pallas_call(functools.partial(kernel, nx, nz, (gx, gy, gz)), out_shape...]
where the time goes in v7:
time: 63.2 us; the launch traced here: 62.1 us
  Pallas kernels  61.5 us (97%)
  between operations  0.64 us (1%)
    pallas_call x1, Pallas kernels, on_device(): pl.pallas_call(functools.partial(kernel, nx, nz, (gx, gy, gz)), out_shape...  59 us
    pallas_call x1, Pallas kernels, on_device(): pl.pallas_call(functools.partial(finish, nx, nz, groups), out_shape=[jax....  2.47 us

profile of v7, /device:TPU:8, one launch (start us, length us, event | category | flops | bytes accessed | tf_op | source)
XLA Modules:
  0.0 62.1 jit_solution(6000069077733328178)
XLA Ops:
  0.6 59.0 %shard_map.50 = (f32[11,34,80,128]{3,2,1,0:T(8,128)S(1)}, f32[32,64,128]{2,1,0:T(8,128)S(1)}, f32[32,8,128]{2,1,0:T(8,128)S(1)}) custom-call(f32[32,64,128]{2,1,0:T(8,128)} %bitcast.5, f32[32,64,128]{2,1,0:T(8,128)} %bitcast.6, f32[32,64,128]{2,1,0:T(8,128)} %bitcast.7), custom_call_target="tpu_custom_call" | custom-call | tf_op jit(solution)/shard_map/pallas_call | solution.py:608
  59.6 2.5 %shard_map.51 = (f32[32,64,128]{2,1,0:T(8,128)}, f32[32,64,128]{2,1,0:T(8,128)}) custom-call(f32[11,34,80,128]{3,2,1,0:T(8,128)S(1)} %get-tuple-element.7.field, f32[32,64,128]{2,1,0:T(8,128)S(1)} %get-tuple-element.8.diag, f32[32,8,128]{2,1,0:T(8,128)S(1)} %get-tuple-element.9.coef), custom_call_target="tpu_custom_call" | custom-call | tf_op jit(solution)/shard_map/pallas_call | solution.py:651

commit v8 on v7

--- a/solution.py
+++ b/solution.py
@@ -18,6 +18,11 @@
     s = a + b
     t = s - a
     return s, (a - (s - t)) + (b - t)
+
+
+def joined_sum(a, b):
+    s, e = two_sum(a[0], b[0])
+    return s, e if a[1] is None else e + (a[1] + b[1])
 
 
 def renew(a, b):
@@ -129,9 +134,9 @@
 
 
 def kernel(nx, nz, sizes, r_hbm, c_hbm, a_hbm, field, diag, coef,
-           cond, absorb, weight, fx, fy, fz, turned, wx, wy, dy, wz, xadd, yadd, zadd, xsend, zsend, zrecv, ysend, yrecv, xrecv,
+           cond, absorb, weight, fx, fy, fz, turned, wx, wy, dy, wz, wzn, zterm, zown, xadd, yadd, zadd, xsend, zsend, zrecv, ysend, yrecv, xrecv,
            part1, part2, dots, table,
-           load_sem, face_send, face_recv, sum1_send, sum1_recv, sum2_send, sum2_recv):
+           load_sem, face_send, face_recv, wz_send, wz_recv, sum1_send, sum1_recv, sum2_send, sum2_recv):
     gx, gy, gz = sizes
     ix, iy, iz = lax.axis_index("gx"), lax.axis_index("gy"), lax.axis_index("gz")
     ox = 1 - ix
@@ -150,6 +155,7 @@
         pltpu.make_async_copy(r_hbm, weight, load_sem.at[2]),
     ]
     loads[0].start()
+    loads[1].start()
 
     zero_face = jnp.zeros((nx, LANES), F32)
     zero_slab = jnp.zeros((nz, LANES), F32)
@@ -171,6 +177,8 @@
                 return 0
 
             lax.fori_loop(0, STEPS + 1, clear_faces, 0)
+            if ref is zrecv:
+                wzn[side] = zero_face
 
     lane = lax.broadcasted_iota(jnp.int32, (half, LANES), 1)
     pair = lane // 2
@@ -233,6 +241,14 @@
         pl.when(iy > 0)(lambda: (yc[0].wait_send(), yc[1].wait_recv())[0])
         pl.when(iy < gy - 1)(lambda: (yc[1].wait_send(), yc[0].wait_recv())[0])
 
+    def weights():
+        return [
+            pltpu.make_async_remote_copy(
+                wz.at[up], wzn.at[1 - up], wz_send.at[up], wz_recv.at[1 - up],
+                device_id=(ix, iy, jnp.clip(iz + 2 * up - 1, 0, gz - 1)), device_id_type=MESH)
+            for up in range(2)
+        ]
+
     def receive_z(e):
         _, _, zc = copies(e)
         pl.when(iz > 0)(lambda: (zc[0].wait_send(), zc[1].wait_recv())[0])
@@ -262,11 +278,10 @@
         part = stage[0]
         for copy in arrivals(stage, which):
             copy.wait_recv()
-        total, error = part[which, 0], jnp.zeros_like(part[which, 0])
-        for i in range(1, part.shape[1]):
-            total, e = two_sum(total, part[which, i])
-            error = error + e
-        return total, error
+        pairs = [(part[which, i], None) for i in range(part.shape[1])]
+        while len(pairs) > 1:
+            pairs = [joined_sum(*pairs[i:i + 2]) for i in range(0, len(pairs), 2)]
+        return pairs[0]
 
     def sum_begin(which, row):
         part1[which, gxy] = row
@@ -357,7 +372,6 @@
         lax.fori_loop(0, nx, add_sides, 0, unroll=4)
 
     loads[0].wait()
-    loads[1].start()
     loads[2].start()
     pl.semaphore_wait(barrier, len(group) + len(line))
     fill_z(cond, 0)
@@ -423,14 +437,20 @@
     xsend[1] = weight[border - 1] / xdiag
     ysend[1] = yright / ydiag
     send_xy(1)
-    sum_middle(0)
     for i in range(2):
         wz[i] = (0.5 * zsend[0, i] + za[i]) / zdiag[i]
+    down, upward = weights()
+    pl.when(iz > 0)(down.start)
+    pl.when(iz < gz - 1)(upward.start)
+    for i in range(2):
+        zterm[i] = zero_face
+        zown[0, i] = zsend[1, i]
     wx[...] = (0.5 * xsend[0] + xa) / xdiag
     sides = (0.5 * ysend[0] + ya) / ydiag
     wy[0] = jnp.where(even, pltpu.roll(sides, LANES - 1, 1), 0.0)
     wy[1] = jnp.where(even, 0.0, pltpu.roll(sides, 1, 1))
     dy[...] = ydiag
+    sum_middle(0)
     keep(za, ya, xa)
     correct(diag, 0, 0)
 
@@ -462,6 +482,18 @@
                 table[j, 0] = kappa
                 table[j, 1] = one
 
+        @pl.when(k == 1)
+        def _():
+            down, upward = weights()
+            pl.when(iz > 0)(lambda: (down.wait_send(), upward.wait_recv())[0])
+            pl.when(iz < gz - 1)(lambda: (upward.wait_send(), down.wait_recv())[0])
+
+        @pl.when(k > 0)
+        def _():
+            before = spread(table[k - 1, 0], half)
+            for i in range(2):
+                zterm[i] = before * wzn[i] * zown[k - 1, i]
+
         correct(field.at[k])
         a = table[k, 0]
         a_all, b_all = spread(a), spread(table[k, 1])
@@ -499,16 +531,18 @@
         high_side = a_half * wy[1] * yrecv[e, 1]
         xa = a_all * wx[...] * xrecv[e]
         zpart = z_edges(zpart, low_side, high_side, xa)
-        zscale = [a_half * wz[i] for i in range(2)]
-        receive_z(e)
-        za = [zscale[i] * zrecv[e, i] for i in range(2)]
 
         @pl.when(k < STEPS - 1)
         def _():
             for i in range(2):
-                zsend[e + 1, i] = zpart[i] + za[i]
+                zsend[e + 1, i] = zpart[i]
             send_z(e + 1)
 
+        zscale = [a_half * wz[i] for i in range(2)]
+        receive_z(e)
+        za = [zscale[i] * (zrecv[e, i] + zterm[i]) for i in range(2)]
+        for i in range(2):
+            zown[k + 1, i] = zpart[i] + za[i]
         ya = joined(low_side, high_side)
         keep(za, ya, xa)
 
@@ -523,7 +557,7 @@
     last = dots[2 * STEPS] + tile_sum(xadd[...] * diag[border - 1] * xsend[STEPS])
     faces = yadd[...] * dy[...] * ysend[STEPS]
     for i in range(2):
-        faces = faces + zadd[i] * diag[pl.ds(0, nx), (nz - 1) * i, :] * zsend[STEPS, i]
+        faces = faces + zadd[i] * diag[pl.ds(0, nx), (nz - 1) * i, :] * zown[STEPS - 1, i]
     sum_begin(2, one_row([last + jnp.sum(faces.reshape(half // 8, 8, LANES), axis=0)]))
     correct(field.at[STEPS])
     sum_middle(1)
@@ -582,7 +616,7 @@
 
     copies = []
     for g in range(groups):
-        lax.fori_loop(g * size, (g + 1) * size, slab, 0, unroll=2)
+        lax.fori_loop(g * size, (g + 1) * size, slab, 0, unroll=4)
         part = pl.ds(g * size, size)
         for n, (src, dst) in enumerate(((xs, x_hbm), (rs, r_hbm))):
             copy = pltpu.make_async_copy(src.at[part], dst.at[part], sems.at[n, g])
@@ -622,6 +656,9 @@
                 pltpu.VMEM((2, nz // 2, LANES), F32),
                 pltpu.VMEM((nz // 2, LANES), F32),
                 pltpu.VMEM((2, nx, LANES), F32),
+                pltpu.VMEM((2, nx, LANES), F32),
+                pltpu.VMEM((2, nx, LANES), F32),
+                pltpu.VMEM((STEPS + 1, 2, nx, LANES), F32),
                 pltpu.VMEM((nz, LANES), F32),
                 pltpu.VMEM((nz // 2, LANES), F32),
                 pltpu.VMEM((2, nx, LANES), F32),
@@ -638,6 +675,8 @@
                 dma((3,)),
                 dma((exchanges, 5)),
                 dma((exchanges, 5)),
+                dma((2,)),
+                dma((2,)),
                 dma((3, gx * gy)),
                 dma((3, gx * gy)),
                 dma((3, gz)),

time: 63.2 us -> 60.3 us (0.954)
  Pallas kernels: 61.5 us -> 58.5 us
    pallas_call x1, Pallas kernels: 59 us -> 56.2 us  [on_device(): pl.pallas_call(functools.partial(kernel, nx, nz, (gx, gy, gz)), out_shape...]
where the time goes in v8:
time: 60.3 us; the launch traced here: 59.2 us
  Pallas kernels  58.5 us (97%)
  between operations  0.64 us (1%)
    pallas_call x1, Pallas kernels, on_device(): pl.pallas_call(functools.partial(kernel, nx, nz, (gx, gy, gz)), out_shape...  56.2 us
    pallas_call x1, Pallas kernels, on_device(): pl.pallas_call(functools.partial(finish, nx, nz, groups), out_shape=[jax....  2.39 us

profile of v8, /device:TPU:8, one launch (start us, length us, event | category | flops | bytes accessed | tf_op | source)
XLA Modules:
  0.0 59.2 jit_solution(5513254687189901290)
XLA Ops:
  0.6 56.2 %shard_map.50 = (f32[11,34,80,128]{3,2,1,0:T(8,128)S(1)}, f32[32,64,128]{2,1,0:T(8,128)S(1)}, f32[32,8,128]{2,1,0:T(8,128)S(1)}) custom-call(f32[32,64,128]{2,1,0:T(8,128)} %bitcast.5, f32[32,64,128]{2,1,0:T(8,128)} %bitcast.6, f32[32,64,128]{2,1,0:T(8,128)} %bitcast.7), custom_call_target="tpu_custom_call" | custom-call | tf_op jit(solution)/shard_map/pallas_call | solution.py:642
  56.8 2.4 %shard_map.51 = (f32[32,64,128]{2,1,0:T(8,128)}, f32[32,64,128]{2,1,0:T(8,128)}) custom-call(f32[11,34,80,128]{3,2,1,0:T(8,128)S(1)} %get-tuple-element.7.field, f32[32,64,128]{2,1,0:T(8,128)S(1)} %get-tuple-element.8.diag, f32[32,8,128]{2,1,0:T(8,128)S(1)} %get-tuple-element.9.coef), custom_call_target="tpu_custom_call" | custom-call | tf_op jit(solution)/shard_map/pallas_call | solution.py:690

commit v9 on v8

--- a/solution.py
+++ b/solution.py
@@ -437,6 +437,7 @@
     xsend[1] = weight[border - 1] / xdiag
     ysend[1] = yright / ydiag
     send_xy(1)
+    sum_middle(0)
     for i in range(2):
         wz[i] = (0.5 * zsend[0, i] + za[i]) / zdiag[i]
     down, upward = weights()
@@ -450,7 +451,6 @@
     wy[0] = jnp.where(even, pltpu.roll(sides, LANES - 1, 1), 0.0)
     wy[1] = jnp.where(even, 0.0, pltpu.roll(sides, 1, 1))
     dy[...] = ydiag
-    sum_middle(0)
     keep(za, ya, xa)
     correct(diag, 0, 0)
 
@@ -460,7 +460,7 @@
         weight[x] = inverse
         return 0
 
-    lax.fori_loop(0, nx, begin, 0, unroll=4)
+    lax.fori_loop(0, nx, begin, 0, unroll=8)
     keep([zero_face, zero_face], jnp.zeros((half, LANES), F32), zero_slab)
 
     def step(k, _):
@@ -494,7 +494,7 @@
             for i in range(2):
                 zterm[i] = before * wzn[i] * zown[k - 1, i]
 
-        correct(field.at[k])
+        pl.when(k > 0)(lambda: correct(field.at[k]))
         a = table[k, 0]
         a_all, b_all = spread(a), spread(table[k, 1])
 
@@ -511,7 +511,7 @@
             w = diag[x] * v
             return same + w * v, older + w * o, ahead + w * new
 
-        same, older, ahead = lax.fori_loop(0, nx, row, (zero_slab, zero_slab, zero_slab), unroll=4)
+        same, older, ahead = lax.fori_loop(0, nx, row, (zero_slab, zero_slab, zero_slab), unroll=8)
         dots[2 * k] = tile_sum(same)
         dots[2 * k + 1] = tile_sum(older)
         dots[2 * STEPS] = tile_sum(ahead)

time: 60.3 us -> 60.1 us (level)
  no operation moved by 1% of the time
where the time goes in v9:
time: 60.1 us; the launch traced here: 59 us
  Pallas kernels  58.4 us (97%)
  between operations  0.64 us (1%)
    pallas_call x1, Pallas kernels, on_device(): pl.pallas_call(functools.partial(kernel, nx, nz, (gx, gy, gz)), out_shape...  56 us
    pallas_call x1, Pallas kernels, on_device(): pl.pallas_call(functools.partial(finish, nx, nz, groups), out_shape=[jax....  2.39 us

profile of v9, /device:TPU:8, one launch (start us, length us, event | category | flops | bytes accessed | tf_op | source)
XLA Modules:
  0.0 59.0 jit_solution(4631175689938637068)
XLA Ops:
  0.6 56.0 %shard_map.50 = (f32[11,34,80,128]{3,2,1,0:T(8,128)S(1)}, f32[32,64,128]{2,1,0:T(8,128)S(1)}, f32[32,8,128]{2,1,0:T(8,128)S(1)}) custom-call(f32[32,64,128]{2,1,0:T(8,128)} %bitcast.5, f32[32,64,128]{2,1,0:T(8,128)} %bitcast.6, f32[32,64,128]{2,1,0:T(8,128)} %bitcast.7), custom_call_target="tpu_custom_call" | custom-call | tf_op jit(solution)/shard_map/pallas_call | solution.py:642
  56.6 2.4 %shard_map.51 = (f32[32,64,128]{2,1,0:T(8,128)}, f32[32,64,128]{2,1,0:T(8,128)}) custom-call(f32[11,34,80,128]{3,2,1,0:T(8,128)S(1)} %get-tuple-element.7.field, f32[32,64,128]{2,1,0:T(8,128)S(1)} %get-tuple-element.8.diag, f32[32,8,128]{2,1,0:T(8,128)S(1)} %get-tuple-element.9.coef), custom_call_target="tpu_custom_call" | custom-call | tf_op jit(solution)/shard_map/pallas_call | solution.py:690

commit v10 on v9

--- a/solution.py
+++ b/solution.py
@@ -332,23 +332,26 @@
     def joined(low_side, high_side):
         return jnp.where(even, pltpu.roll(high_side, LANES - 1, 1), pltpu.roll(low_side, 1, 1))
 
-    def xy_faces(xpart, ypart, za, ya, xa):
-        yface, xface = ypart + ya, xpart + xa
-        xlanes = []
+    def xy_begun(xpart, ypart, ya, xa):
+        yface, xlanes = ypart + ya, []
         for h in range(2):
             here = 2 * nx * h + 1
-            at = half_row == (half - 1) * h
-            moved = jnp.where(face_lane // 2 == face_row + nx * h, pltpu.roll(za[h], here, 1, stride=2, stride_axis=0), 0.0)
-            yface = yface + jnp.where(at, jnp.sum(moved, axis=0, keepdims=True), 0.0)
             xa_half = xa[half * h:half * (h + 1)]
             turns = [(2 * (nx - 1) + here) % LANES, here]
             moved = jnp.where(low_x, pltpu.roll(xa_half, turns[0], 1), pltpu.roll(xa_half, turns[1], 1))
             yface = yface + jnp.where(pair == border - 1 + nx * h, moved, 0.0)
             moved = jnp.where(low_x, pltpu.roll(ya, (LANES - turns[0]) % LANES, 1), pltpu.roll(ya, LANES - turns[1], 1))
             xlanes.append(moved)
+        return xpart + xa + jnp.where(edge, jnp.concatenate(xlanes, axis=0), 0.0), yface
+
+    def xy_ended(xface, yface, za):
+        for h in range(2):
+            at = half_row == (half - 1) * h
+            moved = jnp.where(face_lane // 2 == face_row + nx * h, pltpu.roll(za[h], 2 * nx * h + 1, 1, stride=2, stride_axis=0), 0.0)
+            yface = yface + jnp.where(at, jnp.sum(moved, axis=0, keepdims=True), 0.0)
             z_at = slab_row == (nz - 1) * h
             xface = xface + jnp.where(z_at, jnp.sum(jnp.where(face_row == border - 1, za[h], 0.0), axis=0, keepdims=True), 0.0)
-        return xface + jnp.where(edge, jnp.concatenate(xlanes, axis=0), 0.0), yface
+        return xface, yface
 
     def keep(za, ya, xa):
         yadd[...] = ya
@@ -433,7 +436,7 @@
         zsend[1, i] = zright[i] / zdiag[i]
     send_z(1)
     ya = joined(low_side, high_side)
-    xdiag, ydiag = xy_faces(diag[border - 1], ypart, za, ya, xa)
+    xdiag, ydiag = xy_ended(*xy_begun(diag[border - 1], ypart, ya, xa), za)
     xsend[1] = weight[border - 1] / xdiag
     ysend[1] = yright / ydiag
     send_xy(1)
@@ -538,19 +541,20 @@
                 zsend[e + 1, i] = zpart[i]
             send_z(e + 1)
 
+        ya = joined(low_side, high_side)
+        xface, yface = xy_begun(xpart, ypart, ya, xa)
         zscale = [a_half * wz[i] for i in range(2)]
         receive_z(e)
         za = [zscale[i] * (zrecv[e, i] + zterm[i]) for i in range(2)]
+
+        @pl.when(k < STEPS - 1)
+        def _():
+            xsend[e + 1], ysend[e + 1] = xy_ended(xface, yface, za)
+            send_xy(e + 1)
+
         for i in range(2):
             zown[k + 1, i] = zpart[i] + za[i]
-        ya = joined(low_side, high_side)
         keep(za, ya, xa)
-
-        @pl.when(k < STEPS - 1)
-        def _():
-            xsend[e + 1], ysend[e + 1] = xy_faces(xpart, ypart, za, ya, xa)
-            send_xy(e + 1)
-
         return 0
 
     lax.fori_loop(0, STEPS, step, 0)

time: 60.1 us -> 59.9 us (level)
  no operation moved by 1% of the time
where the time goes in v10:
time: 59.9 us; the launch traced here: 58.8 us
  Pallas kernels  58.2 us (97%)
  between operations  0.64 us (1%)
    pallas_call x1, Pallas kernels, on_device(): pl.pallas_call(functools.partial(kernel, nx, nz, (gx, gy, gz)), out_shape...  55.8 us
    pallas_call x1, Pallas kernels, on_device(): pl.pallas_call(functools.partial(finish, nx, nz, groups), out_shape=[jax....  2.39 us

profile of v10, /device:TPU:8, one launch (start us, length us, event | category | flops | bytes accessed | tf_op | source)
XLA Modules:
  0.0 58.8 jit_solution(14047725156502695454)
XLA Ops:
  0.6 55.8 %shard_map.50 = (f32[11,34,80,128]{3,2,1,0:T(8,128)S(1)}, f32[32,64,128]{2,1,0:T(8,128)S(1)}, f32[32,8,128]{2,1,0:T(8,128)S(1)}) custom-call(f32[32,64,128]{2,1,0:T(8,128)} %bitcast.5, f32[32,64,128]{2,1,0:T(8,128)} %bitcast.6, f32[32,64,128]{2,1,0:T(8,128)} %bitcast.7), custom_call_target="tpu_custom_call" | custom-call | tf_op jit(solution)/shard_map/pallas_call | solution.py:646
  56.4 2.4 %shard_map.51 = (f32[32,64,128]{2,1,0:T(8,128)}, f32[32,64,128]{2,1,0:T(8,128)}) custom-call(f32[11,34,80,128]{3,2,1,0:T(8,128)S(1)} %get-tuple-element.7.field, f32[32,64,128]{2,1,0:T(8,128)S(1)} %get-tuple-element.8.diag, f32[32,8,128]{2,1,0:T(8,128)S(1)} %get-tuple-element.9.coef), custom_call_target="tpu_custom_call" | custom-call | tf_op jit(solution)/shard_map/pallas_call | solution.py:694

commit v11 on v10

--- a/solution.py
+++ b/solution.py
@@ -690,7 +690,7 @@
                 collective_id=0, has_side_effects=True, vmem_limit_bytes=40 * 1024 * 1024
             ),
         )(*[pltpu.with_memory_space_constraint(v, pltpu.HBM) for v in args])
-        groups = 4
+        groups = 8
         out = pl.pallas_call(
             functools.partial(finish, nx, nz, groups),
             out_shape=[jax.ShapeDtypeStruct(block, F32)] * 2,

time: 59.9 us -> 59.9 us (level)
  no operation moved by 1% of the time
where the time goes in v11:
time: 59.9 us; the launch traced here: 58.8 us
  Pallas kernels  58.2 us (97%)
  between operations  0.64 us (1%)
    pallas_call x1, Pallas kernels, on_device(): pl.pallas_call(functools.partial(kernel, nx, nz, (gx, gy, gz)), out_shape...  55.8 us
    pallas_call x1, Pallas kernels, on_device(): pl.pallas_call(functools.partial(finish, nx, nz, groups), out_shape=[jax....  2.41 us

profile of v11, /device:TPU:8, one launch (start us, length us, event | category | flops | bytes accessed | tf_op | source)
XLA Modules:
  0.0 58.8 jit_solution(16839641654953355663)
XLA Ops:
  0.6 55.8 %shard_map.50 = (f32[11,34,80,128]{3,2,1,0:T(8,128)S(1)}, f32[32,64,128]{2,1,0:T(8,128)S(1)}, f32[32,8,128]{2,1,0:T(8,128)S(1)}) custom-call(f32[32,64,128]{2,1,0:T(8,128)} %bitcast.5, f32[32,64,128]{2,1,0:T(8,128)} %bitcast.6, f32[32,64,128]{2,1,0:T(8,128)} %bitcast.7), custom_call_target="tpu_custom_call" | custom-call | tf_op jit(solution)/shard_map/pallas_call | solution.py:646
  56.4 2.4 %shard_map.51 = (f32[32,64,128]{2,1,0:T(8,128)}, f32[32,64,128]{2,1,0:T(8,128)}) custom-call(f32[11,34,80,128]{3,2,1,0:T(8,128)S(1)} %get-tuple-element.7.field, f32[32,64,128]{2,1,0:T(8,128)S(1)} %get-tuple-element.8.diag, f32[32,8,128]{2,1,0:T(8,128)S(1)} %get-tuple-element.9.coef), custom_call_target="tpu_custom_call" | custom-call | tf_op jit(solution)/shard_map/pallas_call | solution.py:694
